TPU v7x, 32 devices: a whole 2x2x4 slice. The times are simulated.
32 devices in a mesh: dp: 16 (over z, y, x), mp: 2 (over core).
Axes of the slice: x: 2, y: 2, z: 4, core: 2. Of those that a mesh axis runs over, the one named last changes fastest.
Arguments:
- tokens: bfloat16 [192, 196, 512], P('dp'), may hold values from -6 to 6
- cotangent: float32 [192, 196, 512], P('dp'), may hold values from -6 to 6
- image_count: int32 [16], P('dp'), may hold values from 1 to 12, as said below
- rel_index: int32 [49, 49], replicated, may hold values from 0 to 168, as said below
- w_qkv: float32 [2, 512, 3, 512], P(None, 'dp', None, 'mp'), may hold values from -0.25 to 0.25
- w_proj: float32 [2, 512, 512], P(None, 'mp', 'dp'), may hold values from -0.5 to 0.5
- w_fc_one: float32 [2, 512, 2048], P(None, 'dp', 'mp'), may hold values from -0.25 to 0.25
- w_fc_two: float32 [2, 2048, 512], P(None, 'mp', 'dp'), may hold values from -0.125 to 0.125
- qv_bias: float32 [2, 2, 512], P(None, None, 'mp'), may hold values from -3 to 3
- fc_one_bias: float32 [2, 2048], P(None, 'mp'), may hold values from -3 to 3
- rel_table: float32 [2, 169, 16], P(None, None, 'mp'), may hold values from -4 to 4
- norm_vec: float32 [2, 6, 512], replicated, may hold values from 0.1 to 1.9
- m_qkv: float32 [2, 512, 3, 512], P(None, 'dp', None, 'mp'), may hold values from -40 to 40
- m_proj: float32 [2, 512, 512], P(None, 'mp', 'dp'), may hold values from -40 to 40
- m_fc_one: float32 [2, 512, 2048], P(None, 'dp', 'mp'), may hold values from -40 to 40
- m_fc_two: float32 [2, 2048, 512], P(None, 'mp', 'dp'), may hold values from -40 to 40
- m_qv_bias: float32 [2, 2, 512], P(None, None, 'mp'), may hold values from -40 to 40
- m_fc_one_bias: float32 [2, 2048], P(None, 'mp'), may hold values from -40 to 40
- m_rel_table: float32 [2, 169, 16], P(None, None, 'mp'), may hold values from -40 to 40
- m_norm_vec: float32 [2, 6, 512], replicated, may hold values from -40 to 40
- v_qkv: float32 [2, 512, 3, 512], P(None, 'dp', None, 'mp'), may hold values from 3.7632 to 37.632
- v_proj: float32 [2, 512, 512], P(None, 'mp', 'dp'), may hold values from 3.7632 to 37.632
- v_fc_one: float32 [2, 512, 2048], P(None, 'dp', 'mp'), may hold values from 3.7632 to 37.632
- v_fc_two: float32 [2, 2048, 512], P(None, 'mp', 'dp'), may hold values from 3.7632 to 37.632
- v_qv_bias: float32 [2, 2, 512], P(None, None, 'mp'), may hold values from 3.7632 to 37.632
- v_fc_one_bias: float32 [2, 2048], P(None, 'mp'), may hold values from 3.7632 to 37.632
- v_rel_table: float32 [2, 169, 16], P(None, None, 'mp'), may hold values from 3.7632 to 37.632
- v_norm_vec: float32 [2, 6, 512], replicated, may hold values from 3.7632 to 37.632
Outputs:
- out: float32 [192, 196, 512], P('dp')
- x_grad: float32 [192, 196, 512], P('dp')
- new_w_qkv: float32 [2, 512, 3, 512], P(None, 'dp', None, 'mp')
- new_w_proj: float32 [2, 512, 512], P(None, 'mp', 'dp')
- new_w_fc_one: float32 [2, 512, 2048], P(None, 'dp', 'mp')
- new_w_fc_two: float32 [2, 2048, 512], P(None, 'mp', 'dp')
- new_qv_bias: float32 [2, 2, 512], P(None, None, 'mp')
- new_fc_one_bias: float32 [2, 2048], P(None, 'mp')
- new_rel_table: float32 [2, 169, 16], P(None, None, 'mp')
- new_norm_vec: float32 [2, 6, 512], replicated
- new_m_qkv: float32 [2, 512, 3, 512], P(None, 'dp', None, 'mp')
- new_m_proj: float32 [2, 512, 512], P(None, 'mp', 'dp')
- new_m_fc_one: float32 [2, 512, 2048], P(None, 'dp', 'mp')
- new_m_fc_two: float32 [2, 2048, 512], P(None, 'mp', 'dp')
- new_m_qv_bias: float32 [2, 2, 512], P(None, None, 'mp')
- new_m_fc_one_bias: float32 [2, 2048], P(None, 'mp')
- new_m_rel_table: float32 [2, 169, 16], P(None, None, 'mp')
- new_m_norm_vec: float32 [2, 6, 512], replicated
- new_v_qkv: float32 [2, 512, 3, 512], P(None, 'dp', None, 'mp')
- new_v_proj: float32 [2, 512, 512], P(None, 'mp', 'dp')
- new_v_fc_one: float32 [2, 512, 2048], P(None, 'dp', 'mp')
- new_v_fc_two: float32 [2, 2048, 512], P(None, 'mp', 'dp')
- new_v_qv_bias: float32 [2, 2, 512], P(None, None, 'mp')
- new_v_fc_one_bias: float32 [2, 2048], P(None, 'mp')
- new_v_rel_table: float32 [2, 169, 16], P(None, None, 'mp')
- new_v_norm_vec: float32 [2, 6, 512], replicated
Inputs may be any that keep to these rules, and one draw needn't show every extreme that they name: `image_count`: slots below a device's count hold live images; some index of dp holds 12. `rel_index`: pairs of window positions with the same relative offset share one entry; distinct offsets have distinct entries.
All inputs are finite; a program needn't handle non-finite values.
Results may differ from a plain program's by a relative error of at most 0.023.
Values may be sent and summed in bfloat16 or wider, within the bound.
A program may use at most 320 MiB of HBM per device.

v0:
```python
import functools

import jax
import jax.numpy as jnp
import numpy as np
from jax import lax
from jax.experimental import pallas as pl
from jax.experimental.pallas import tpu as pltpu
from jax.sharding import PartitionSpec as P

D = 512
HD = 32
SIDE = 14
WIN = 7
SHIFT = 3
SEQ = 196
WSEQ = 49
TABLE = 169
LAYERS = 2
SEQP = 200
PAIR = 2
ROWS = PAIR * SEQP
WROW = 64
WIMG = 4 * WROW
WPAIR = PAIR * WIMG
HALF = 256
GROUP = 4
GROUPS = 4
QUAD = GROUP * HD
LANES = GROUP * WROW
FFH = 1024
QKV = 3 * HALF
COLS = 2 * FFH + QKV + HALF
ATT = 2 * FFH

norm_eps = 1e-05
mask_fill = -100.0
pad_fill = -1e30
beta_one = 0.9
beta_two = 0.999
adam_eps = 1e-08
learn_rate = 0.02
decay_rate = 0.05
adam_step = 3.0
root_half = 0.7071067811865476
inv_root_two_pi = 0.3989422804014327
score_scale = HD**-0.5
log2_e = 1.4426950408889634

f32 = jnp.float32
bf16 = jnp.bfloat16


def dot(a, b, ca=1, cb=0):
    return lax.dot_general(a, b, (((ca,), (cb,)), ((), ())), preferred_element_type=f32)


def window_tokens(shifted):
    off = SHIFT if shifted else 0
    out = np.zeros((4, WSEQ), np.int64)
    for wr in range(2):
        for wc in range(2):
            for p in range(WSEQ):
                r = (7 * wr + p // 7 + off) % SIDE
                c = (7 * wc + p % 7 + off) % SIDE
                out[wr * 2 + wc, p] = r * SIDE + c
    return out


def permutation(shifted):
    tok = window_tokens(shifted)
    perm = np.zeros((WIMG, SEQP), np.float32)
    for w in range(4):
        perm[w * WROW + np.arange(WSEQ), tok[w]] = 1.0
    return perm


def region_mask():
    pos = np.arange(SIDE)
    band = (pos >= SIDE - WIN).astype(int) + (pos >= SIDE - SHIFT).astype(int)
    region = 3 * band[:, None] + band[None, :]
    win = region.reshape(2, WIN, 2, WIN).transpose(0, 2, 1, 3).reshape(4, WSEQ)
    out = np.zeros((4, WROW, WROW), np.float32)
    out[:, :WSEQ, :WSEQ] = np.where(win[:, :, None] != win[:, None, :], mask_fill, 0.0)
    return out


def norm_stats(z):
    mean = jnp.mean(z, -1, keepdims=True)
    cen = z - mean
    var = jnp.mean(cen * cen, -1, keepdims=True)
    inv = lax.rsqrt(var + norm_eps)
    return cen * inv, inv


def norm_back(e, hat, inv, gain):
    s = e * gain
    return inv * (s - jnp.mean(s, -1, keepdims=True) - hat * jnp.mean(s * hat, -1, keepdims=True))


def row_sum(v):
    return jnp.sum(v, 0, keepdims=True)


def put_images(ref, rows, blk, scale=lambda im, v: v):
    part = ref.at[rows, :]
    for im in range(PAIR):
        part[im * SEQP : im * SEQP + SEQ, :] = scale(im, blk[im].astype(f32))
        part[im * SEQP + SEQ : (im + 1) * SEQP, :] = jnp.zeros((SEQP - SEQ, D), f32)


def flat(v):
    return v.reshape(D, v.shape[-1])


def to_window_rows(perm, rows, out_ref):
    for im in range(PAIR):
        part = rows[im * SEQP : (im + 1) * SEQP].astype(bf16)
        out_ref[im * WIMG : (im + 1) * WIMG, :] = dot(perm, part).astype(bf16)


def to_token_rows(perm_t, ref):
    return jnp.concatenate(
        [dot(perm_t, ref[im * WIMG : (im + 1) * WIMG, :]) for im in range(PAIR)], 0
    ).astype(bf16)


def expand_heads(x, hm_ref):
    return jnp.concatenate([x * hm_ref[h : h + 1, :] for h in range(GROUP)], 0)


def fold_heads(o):
    lane = lax.broadcasted_iota(jnp.int32, (WROW, QUAD), 1) // HD
    acc = o[:WROW]
    for h in range(1, GROUP):
        acc = jnp.where(lane == h, o[h * WROW : (h + 1) * WROW], acc)
    return acc


def staged(stages, count, lag, at):
    for t in range(count + lag * (len(stages) - 1)):
        if t > 0 and t % SPAN == 0 and t // SPAN <= 2:
            at("attend", 2 + t // SPAN)
        for n, stage in enumerate(stages):
            if 0 <= t - lag * n < count:
                stage(t - lag * n)


def softmax_cols(s):
    e = jnp.exp2((s - jnp.max(s, 0, keepdims=True)) * (score_scale * log2_e))
    return e * (1.0 / jnp.sum(e, 0, keepdims=True))


def group_cols(g):
    base = (g // 2) * QKV + (g % 2) * QUAD
    return [slice(base + t * HALF, base + t * HALF + QUAD) for t in range(3)]


def attend_forward(x, wa, bias_ref, layer, vec_ref, nv_ref, perm, perm_t, hm_ref, qkv_ref, mixed_ref,
                   nperm, mixw, sc, prc, at):
    hat, _ = norm_stats(x)
    normed = hat * nv_ref[0:1, :] + nv_ref[1:2, :]
    to_window_rows(perm, normed, nperm)
    for m in range(2):
        r = dot(nperm[...], flat(wa[m, ..., :QKV]))
        base = m * QKV
        qkv_ref[:, base : base + HALF] = (r[:, :HALF] + vec_ref[m, layer, 1:2, :HALF]).astype(bf16)
        qkv_ref[:, base + HALF : base + 2 * HALF] = r[:, HALF : 2 * HALF].astype(bf16)
        qkv_ref[:, base + 2 * HALF : base + QKV] = (r[:, 2 * HALF :] + vec_ref[m, layer, 2:3, :HALF]).astype(bf16)
    at("attend", 1)
    units = [(w, g) for w in range(4 * PAIR) for g in range(GROUPS)]

    def scores(t):
        w, g = units[t]
        r = slice(w * WROW, (w + 1) * WROW)
        cq, ck, _ = group_cols(g)
        sc[t % SLOTS] = dot(qkv_ref[r, ck], expand_heads(qkv_ref[r, cq], hm_ref), 1, 1) + bias_ref[g // 2, layer * (1 + w % 4), g % 2]

    def middle(t):
        prc[t % SLOTS] = softmax_cols(sc[t % SLOTS]).astype(bf16)

    def mix(t):
        w, g = units[t]
        r = slice(w * WROW, (w + 1) * WROW)
        o = dot(prc[t % SLOTS], qkv_ref[r, group_cols(g)[2]], 0, 0)
        mixw[r, g * QUAD : (g + 1) * QUAD] = fold_heads(o).astype(bf16)

    staged((scores, middle, mix), len(units), LAG, at)
    mixed = to_token_rows(perm_t, mixw)
    mixed_ref[...] = mixed
    attn = dot(mixed[:, :HALF], flat(wa[0, ..., QKV:]), 1, 1) + dot(mixed[:, HALF:], flat(wa[1, ..., QKV:]), 1, 1)
    return x + attn + nv_ref[4:5, :]


CH = 512
SLOTS = 8
LAG = 2
SPAN = 12


def mlp_forward(mid, wm, vec_ref, layer, nv_ref, act_ref, slope_ref, at):
    hat, _ = norm_stats(mid)
    hid = (hat * nv_ref[2:3, :] + nv_ref[3:4, :]).astype(bf16)
    total = jnp.zeros((ROWS, D), f32)
    for m in range(2):
        for c in range(0, FFH, CH):
            col = m * FFH + c
            u = dot(hid, flat(wm[m, ..., c : c + CH])) + vec_ref[m, layer, 0:1, c : c + CH]
            t = u * root_half
            phi = 0.5 + 0.5 * lax.erf(t)
            act = (u * phi).astype(bf16)
            act_ref[:, col : col + CH] = act
            slope_ref[:, col : col + CH] = (phi + u * (jnp.exp2(t * t * -log2_e) * inv_root_two_pi)).astype(bf16)
            if col > 0:
                at("mlp", col // CH)
            total += dot(act, flat(wm[m, ..., FFH + c : FFH + c + CH]), 1, 1)
    return mid + total + nv_ref[5:6, :]


def mlp_backward(g_s, mid, wm, nv_ref, gp, hid_s, gb_s, rows, b1_acc, nv_acc, at):
    gout = g_s[rows, :]
    hat, inv = norm_stats(mid)
    hid_s[rows, :] = (hat * nv_ref[2:3, :] + nv_ref[3:4, :]).astype(bf16)
    gb = gout.astype(bf16)
    gb_s[rows, :] = gb
    ghid = jnp.zeros((ROWS, D), f32)
    for m in range(2):
        for c in range(0, FFH, CH):
            col = m * FFH + c
            g = dot(gb, flat(wm[m, ..., FFH + c : FFH + c + CH])) * gp[rows, col : col + CH].astype(f32)
            b1_acc[:, col : col + CH] += row_sum(g)
            g = g.astype(bf16)
            gp[rows, col : col + CH] = g
            if col > 0:
                at("mlp", col // CH)
            ghid += dot(g, flat(wm[m, ..., c : c + CH]), 1, 1)
    gmid = gout + norm_back(ghid, hat, inv, nv_ref[2:3, :])
    nv_acc[2:3, :] += row_sum(ghid * hat)
    nv_acc[3:4, :] += row_sum(ghid)
    nv_acc[4:5, :] += row_sum(gmid)
    nv_acc[5:6, :] += row_sum(gout)
    g_s[rows, :] = gmid


def attend_backward(g_s, x, wa, bias_ref, layer, nv_ref, perm, perm_t, hm_ref, qkv_ref,
                    mperm, gmw, gqw, gq_s, mb_s, nb_s, rows, ds_acc, qv_acc, nv_acc, sc, dpc, prc, dsc, at):
    gmid = g_s[rows, :]
    hat, inv = norm_stats(x)
    nb_s[rows, :] = (hat * nv_ref[0:1, :] + nv_ref[1:2, :]).astype(bf16)
    mb_s[rows, :] = gmid.astype(bf16)
    to_window_rows(perm, gmid, mperm)
    for m in range(2):
        gmw[:, m * HALF : (m + 1) * HALF] = dot(mperm[...], flat(wa[m, ..., QKV:])).astype(bf16)
    at("attend", 1)
    units = [(w, g) for w in range(4 * PAIR) for g in range(GROUPS)]

    def scores(t):
        w, g = units[t]
        r = slice(w * WROW, (w + 1) * WROW)
        cq, ck, cv = group_cols(g)
        sc[t % SLOTS] = dot(qkv_ref[r, ck], expand_heads(qkv_ref[r, cq], hm_ref), 1, 1) + bias_ref[g // 2, layer * (1 + w % 4), g % 2]
        dpc[t % SLOTS] = dot(qkv_ref[r, cv], expand_heads(gmw[r, g * QUAD : (g + 1) * QUAD], hm_ref), 1, 1)

    def middle(t):
        g = units[t][1]
        pr = softmax_cols(sc[t % SLOTS])
        prc[t % SLOTS] = pr.astype(bf16)
        dp = dpc[t % SLOTS]
        ds = pr * (dp - jnp.sum(pr * dp, 0, keepdims=True))
        ds_acc[g] += ds
        dsc[t % SLOTS] = ds.astype(bf16)

    def grads(t):
        w, g = units[t]
        r = slice(w * WROW, (w + 1) * WROW)
        cq, ck, cv = group_cols(g)
        own = slice(g * QUAD, (g + 1) * QUAD)
        gv = dot(prc[t % SLOTS], expand_heads(gmw[r, own], hm_ref))
        gk = dot(dsc[t % SLOTS], expand_heads(qkv_ref[r, cq], hm_ref)) * score_scale
        gq = fold_heads(dot(dsc[t % SLOTS], qkv_ref[r, ck], 0, 0)) * score_scale
        qv_acc[0:1, own] += row_sum(gq)
        qv_acc[1:2, own] += row_sum(gv)
        gqw[r, cq] = gq.astype(bf16)
        gqw[r, ck] = gk.astype(bf16)
        gqw[r, cv] = gv.astype(bf16)

    staged((scores, middle, grads), len(units), LAG, at)
    at("attend", 2)
    gq = to_token_rows(perm_t, gqw)
    gq_s[rows, :] = gq
    gnorm = dot(gq[:, :QKV], flat(wa[0, ..., :QKV]), 1, 1) + dot(gq[:, QKV:], flat(wa[1, ..., :QKV]), 1, 1)
    nv_acc[0:1, :] += row_sum(gnorm * hat)
    nv_acc[1:2, :] += row_sum(gnorm)
    g_s[rows, :] = g_s[rows, :] + norm_back(gnorm, hat, inv, nv_ref[0:1, :])


def forward_kernel(fast, steps, tok_ref, *refs):
    shards, refs = refs[: 4 if fast else 2], refs[4 if fast else 2 :]
    (bias_in, vec_in, nv_ref, perm_ref, perm_t_ref, hm_ref,
     out_ref, ys_ref, mid_ref, qkv_ref, mixed_ref, act_ref, slope_ref, wa_out, wm_out, bias_out,
     xs, mids, wa, wm, nperm, mixw, sc, prc, bias_ref, vec_ref, local, *sems) = refs
    s = pl.program_id(0)
    per = 2 * steps
    layer, r = s // per, lax.rem(s, per)
    pair = lax.rem(r, steps)
    rows = pl.ds(pl.multiple_of(pair * ROWS, ROWS), ROWS)
    weights = (wa, wm)
    me = lax.axis_index("mp")
    if fast:
        send, recv, own_a, own_m, ssend, srecv = sems
        own = (own_a, own_m)
        swaps = [
            remote(here, there.at[me], ssend.at[n], srecv.at[n], Place().core())
            for n, (here, there) in enumerate(((bias_in, bias_ref), (vec_in, vec_ref)))
        ]
        gathers = [
            Gather(own[n % 2].at[n // 2], weights[n % 2].at[n // 2], send.at[n], recv.at[n], local.at[n])
            for n in range(2 * LAYERS)
        ]

    def keep(n):
        return pltpu.make_async_copy(weights[n % 2].at[n // 2], (wa_out, wm_out)[n % 2].at[n // 2], local.at[4 + n])

    def at(step, point):
        if not fast:
            return
        for key, todo in FORWARD_PLAN.items():
            if key[1] == point and (key[0] % per < steps) == (step == "attend"):

                @pl.when(s == key[0])
                def _():
                    for n, stage in todo:
                        gathers[n].stage(stage)
                        if stage == Gather.STAGES - 1:
                            keep(n).start()

    keep_bias = pltpu.make_async_copy(bias_ref, bias_out, local.at[8])

    @pl.when(s == 0)
    def _():
        if fast:
            pack_shards(shards, own_a, own_m)
            neighbour_barrier(Place())
            for swap in swaps:
                swap.start()
        else:
            for n in range(2 * LAYERS):
                cp = pltpu.make_async_copy(shards[n % 2].at[n // 2], weights[n % 2].at[n // 2], local.at[n])
                cp.start()
                cp.wait()
            for here, there in ((bias_in, bias_ref), (vec_in, vec_ref)):
                there[...] = here[...]

    at("attend", 0)

    @pl.when(s == 0)
    def _():
        if fast:
            for here, there in ((bias_in, bias_ref), (vec_in, vec_ref)):
                there[me] = here[...]
            for swap in swaps:
                swap.wait()
        keep_bias.start()

    @pl.when(r < steps)
    def _():
        @pl.when(s < steps)
        def _():
            put_images(xs, rows, tok_ref)

        mid = attend_forward(xs[rows, :], wa.at[layer], bias_ref, layer, vec_ref, nv_ref.at[layer],
                             perm_ref[layer], perm_t_ref[layer], hm_ref, qkv_ref, mixed_ref, nperm, mixw, sc, prc, at)
        mid_ref[...] = mid
        mids[rows, :] = mid
        at("attend", 2)

    @pl.when(r >= steps)
    def _():
        at("mlp", 0)
        y = mlp_forward(mids[rows, :], wm.at[layer], vec_ref, layer, nv_ref.at[layer], act_ref, slope_ref, at)

        @pl.when(layer < LAYERS - 1)
        def _():
            xs[rows, :] = y
            ys_ref[...] = y

        @pl.when(layer == LAYERS - 1)
        def _():
            for im in range(PAIR):
                part = y[im * SEQP : im * SEQP + SEQ]
                out_ref[im] = part

    @pl.when(s == LAYERS * per - 1)
    def _():
        keep_bias.wait()
        if fast:
            for n in range(2 * LAYERS):
                keep(n).wait()


def pack_shards(shards, own_a, own_m):
    w_qkv, w_proj, w_one, w_two = shards
    for l in range(LAYERS):
        for k in range(3):
            own_a[l, :, k * HALF : (k + 1) * HALF] = w_qkv[l, k].astype(bf16)
        own_a[l, :, QKV:] = w_proj[l].astype(bf16)
        own_m[l, :, :FFH] = w_one[l].astype(bf16)
        own_m[l, :, FFH:] = w_two[l].astype(bf16)


FORWARD_PLAN = {
    (0, 0): [(0, 0), (1, 0), (0, 1), (0, 2), (0, 3), (1, 1), (0, 4), (1, 2), (1, 3), (0, 5), (0, 6)],
    (1, 1): [(1, 4)],
    (2, 1): [(1, 5)],
    (3, 0): [(2, 0), (1, 6)],
    (3, 2): [(2, 1)],
    (4, 0): [(2, 2)],
    (4, 1): [(2, 3), (3, 0)],
    (4, 3): [(2, 4)],
    (5, 0): [(3, 1)],
    (5, 1): [(2, 5), (3, 2)],
    (6, 0): [(2, 6)],
    (6, 1): [(3, 3)],
    (7, 1): [(3, 4)],
    (8, 1): [(3, 5)],
    (9, 0): [(3, 6)],
}


def backward_kernel(fast, steps, cot_ref, tok_ref, ys_ref, mid_ref, qkv_ref, act_in, slope_in, mixed_in, wa_in, wm_in,
                    bias_ref, nv_ref, perm_ref, perm_t_ref, hm_ref, count_ref, *refs):
    if fast:
        gx_ref, ga_out, sum_m, sum_a, *refs = refs
    else:
        gx_ref, ga_out, gm_out, *refs = refs
    (qv_all, b1_all, ds_all, nv_all, g_s, xs, mperm, gmw, gqw, gp, gq_s, hid_s, gb_s, mb_s, nb_s, act_s, mixed_s,
     wa, wm, gwm, gwa, sc, dpc, prc, dsc, local, *comm) = refs
    s = pl.program_id(0)
    per = 2 * steps + 6
    turn, r = s // per, lax.rem(s, per)
    layer = LAYERS - 1 - turn
    first_g, first_a, last_g = steps, steps + 4, 2 * steps + 4
    pair = jnp.where(r < first_a, jnp.minimum(r, steps - 1), jnp.minimum(r - first_a, steps - 1))
    rows = pl.ds(pl.multiple_of(pair * ROWS, ROWS), ROWS)
    total = steps * ROWS
    qv_acc, b1_acc, ds_acc, nv_acc, nv_ref = (
        ref.at[layer] for ref in (qv_all, b1_all, ds_all, nv_all, nv_ref)
    )
    me = lax.axis_index("mp")
    if fast:
        scatters = [
            Scatter(gw.at[0], gw.at[1], *comm[8 * n : 8 * n + 8]) for n, gw in enumerate((gwm.at[0], gwm.at[1], gwa))
        ]
        pl.when(s == 0)(lambda: neighbour_barrier(Place()))

    def at(step, point):
        if not fast:
            return
        spans = {"mlp": (0, first_g), "g": (first_g, first_a), "attend": (first_a, last_g), "ga": (last_g, per)}
        for key, todo in BACKWARD_PLAN.items():
            lo, hi = spans[step]
            if key[1] == point and lo <= key[0] % per < hi:

                @pl.when(s == key[0])
                def _():
                    for n, stage in todo:
                        if stage == Scatter.STAGES - 1:
                            last = key[0] < per + first_a
                            scatters[n].result(sum_a.at[0] if n == 2 else sum_m.at[n, LAYERS - 1 if last else 0])
                        scatters[n].stage(stage)

    def rows_of(l):
        return pl.ds(l * total, total)

    def load(name, l):
        src, dst, n = {
            "wm": (wm_in.at[l], wm, 0), "wa": (wa_in.at[l], wa, 1), "act": (act_in.at[rows_of(l)], act_s, 2),
            "mixed": (mixed_in.at[rows_of(l)], mixed_s, 3), "slope": (slope_in.at[rows_of(l)], gp, 4),
        }[name]
        return pltpu.make_async_copy(src, dst, local.at[n])

    top = LAYERS - 1

    @pl.when(s == 0)
    def _():
        for name in ("wm", "slope", "wa", "act", "mixed"):
            load(name, top).start()

    for l in range(top, -1, -1):
        base = (top - l) * per
        for name, step in (("wm", 0), ("slope", 0), ("act", first_g), ("wa", first_a), ("mixed", last_g)):
            pl.when(s == base + step)(lambda name=name, l=l: load(name, l).wait())
        if l > 0:
            for name, step in (("wm", first_g), ("slope", first_a), ("act", first_a), ("wa", last_g), ("mixed", per)):
                pl.when(s == base + step)(lambda name=name, l=l: load(name, l - 1).start())

    @pl.when(r == 0)
    def _():
        for ref in (qv_acc, b1_acc, ds_acc, nv_acc):
            ref[...] = jnp.zeros(ref.shape, f32)

    @pl.when(r < first_g)
    def _():
        at("mlp", 0)

        @pl.when(turn == 0)
        def _():
            image = (me * steps + pair) * PAIR
            put_images(g_s, rows, cot_ref, lambda im, v: v * (image + im < count_ref[0]).astype(f32))

        mlp_backward(g_s, mid_ref[...], wm, nv_ref, gp, hid_s, gb_s, rows, b1_acc, nv_acc, at)

    def gradient(left, right, lo, width):
        cols = pl.ds(pl.multiple_of(lo, width), width)
        return dot(left[...], right[:, cols], 0, 0).astype(bf16).reshape(*gwa.shape[1:-1], width)

    @pl.when((r >= first_g) & (r < first_a))
    def _():
        at("g", 0)
        q = r - first_g
        own = lax.rem(q, 2)
        half = jnp.where(own == 1, me, 1 - me)

        @pl.when(q < 2)
        def _():
            gwm[0, own] = gradient(hid_s, gp, half * FFH, FFH)

        @pl.when(q >= 2)
        def _():
            gwm[1, own] = gradient(gb_s, act_s, half * FFH, FFH)

        at("g", 1)

    @pl.when((r >= first_a) & (r < last_g))
    def _():
        at("attend", 0)

        @pl.when(layer == 0)
        def _():
            put_images(xs, slice(None), tok_ref)

        @pl.when(layer > 0)
        def _():
            xs[...] = ys_ref[...]

        attend_backward(g_s, xs[...], wa, bias_ref, layer, nv_ref, perm_ref[layer], perm_t_ref[layer], hm_ref,
                        qkv_ref, mperm, gmw, gqw, gq_s, mb_s, nb_s, rows, ds_acc, qv_acc, nv_acc, sc, dpc, prc, dsc, at)

        @pl.when(layer == 0)
        def _():
            for im in range(PAIR):
                part = g_s.at[rows, :][im * SEQP : im * SEQP + SEQ]
                gx_ref[im] = part

    @pl.when(r >= last_g)
    def _():
        at("ga", 0)
        own = r - last_g
        half = jnp.where(own == 1, me, 1 - me)
        gwa[own, ..., :QKV] = gradient(nb_s, gq_s, half * QKV, QKV)
        gwa[own, ..., QKV:] = gradient(mb_s, mixed_s, half * HALF, HALF)
        at("ga", 1)

    def flush(src, dst):
        cp = pltpu.make_async_copy(src, dst, local.at[5])
        cp.start()
        cp.wait()

    if fast:
        pl.when(s == LAYERS * per - 1)(lambda: flush(gwa, ga_out))
    else:
        pl.when(r == first_a)(lambda: flush(gwm, gm_out.at[layer]))
        pl.when(r == per - 1)(lambda: flush(gwa, ga_out.at[layer]))


BACKWARD_PLAN = {
    (4, 0): [(0, 0)],
    (5, 0): [(0, 1)],
    (6, 0): [(1, 0)],
    (7, 0): [(1, 1)],
    (7, 4): [(0, 2)],
    (8, 1): [(0, 3)],
    (8, 2): [(1, 2)],
    (9, 4): [(1, 3)],
    (10, 0): [(0, 4)],
    (11, 0): [(2, 0)],
    (12, 0): [(2, 1)],
    (13, 0): [(1, 4)],
    (13, 3): [(2, 2)],
    (14, 3): [(2, 3)],
    (16, 0): [(0, 0)],
    (17, 0): [(2, 4), (0, 1)],
    (18, 0): [(1, 0)],
    (19, 0): [(1, 1)],
    (19, 4): [(0, 2)],
    (20, 1): [(0, 3)],
    (20, 2): [(1, 2)],
    (21, 4): [(1, 3)],
    (22, 0): [(0, 4)],
    (23, 1): [(1, 4)],
}


def whole(shape, buffers=1):
    zero = (0,) * len(shape)
    return pl.BlockSpec(shape, lambda i: zero, pipeline_mode=pl.Buffered(buffers))


VLIM = 65000000


def forward(tok, shards, bias, vecs, nv, perm, perm_t, hm, fast, steps):
    per = 2 * steps
    rows = steps * ROWS
    slots = (2, NZ, NY, NX, D // PEERS) if fast else (2, 1, 1, 1, D)
    wide = (COLS - ATT, ATT)
    any_ = pl.BlockSpec(memory_space=pl.ANY)

    def attend(s):
        return s // per * steps + jnp.minimum(lax.rem(s, per), steps - 1)

    def mlp(s):
        return s // per * steps + jnp.maximum(lax.rem(s, per) - steps, 0)

    sems = []
    if fast:
        sems = [pltpu.SemaphoreType.DMA((2 * LAYERS, Gather.SEMS))] * 2
        sems += [pltpu.VMEM((LAYERS, D // PEERS, n), bf16) for n in wide] + [pltpu.SemaphoreType.DMA((2,))] * 2
    halves = [(2, *a.shape) if fast else a.shape for a in (bias, vecs)]
    params = dict(collective_id=1, has_side_effects=True) if fast else {}
    return pl.pallas_call(
        functools.partial(forward_kernel, fast, steps),
        name="forward",
        grid=(LAYERS * per,),
        in_specs=[
            pl.BlockSpec((PAIR, SEQ, D), lambda s: (lax.axis_index("mp") * steps + jnp.minimum(s, steps - 1), 0, 0)),
            *(whole(w.shape) if fast else any_ for w in shards),
            *(whole(a.shape) for a in (bias, vecs, nv, perm, perm_t, hm)),
        ],
        out_specs=[
            pl.BlockSpec((PAIR, SEQ, D), lambda s: (jnp.maximum(s - (LAYERS * per - steps), 0), 0, 0)),
            pl.BlockSpec((ROWS, D), lambda s: (jnp.clip(s - steps, 0, steps - 1), 0)),
            pl.BlockSpec((ROWS, D), lambda s: (attend(s), 0)),
            pl.BlockSpec((WPAIR, 2 * QKV), lambda s: (attend(s), 0)),
            pl.BlockSpec((ROWS, D), lambda s: (attend(s), 0)),
            pl.BlockSpec((ROWS, 2 * FFH), lambda s: (mlp(s), 0)),
            pl.BlockSpec((ROWS, 2 * FFH), lambda s: (mlp(s), 0)),
            any_, any_, any_,
        ],
        out_shape=[
            jax.ShapeDtypeStruct((steps * PAIR, SEQ, D), f32),
            jax.ShapeDtypeStruct((rows, D), f32),
            jax.ShapeDtypeStruct((LAYERS * rows, D), f32),
            jax.ShapeDtypeStruct((LAYERS * steps * WPAIR, 2 * QKV), bf16),
            jax.ShapeDtypeStruct((LAYERS * rows, D), bf16),
            jax.ShapeDtypeStruct((LAYERS * rows, 2 * FFH), bf16),
            jax.ShapeDtypeStruct((LAYERS * rows, 2 * FFH), bf16),
            *(jax.ShapeDtypeStruct((LAYERS, *slots, n), bf16) for n in wide),
            jax.ShapeDtypeStruct(halves[0], f32),
        ],
        scratch_shapes=[
            pltpu.VMEM((rows, D), f32), pltpu.VMEM((rows, D), f32),
            *(pltpu.VMEM((LAYERS, *slots, n), bf16) for n in wide),
            pltpu.VMEM((WPAIR, D), bf16), pltpu.VMEM((WPAIR, D), bf16),
            pltpu.VMEM((SLOTS, WROW, LANES), f32), pltpu.VMEM((SLOTS, WROW, LANES), bf16),
            *(pltpu.VMEM(n, f32) for n in halves),
            pltpu.SemaphoreType.DMA((9,)), *sems,
        ],
        compiler_params=pltpu.CompilerParams(vmem_limit_bytes=VLIM, **params),
    )(tok, *shards, bias, vecs, nv, perm, perm_t, hm)


def backward(cot, tok, saved, weights, bias, nv, perm, perm_t, hm, count, fast, steps):
    ys, mid, qkv, mixed, act, slope = saved
    wa, wm = weights
    per = 2 * steps + 6
    rows = steps * ROWS
    slots = wa.shape[1:-1]
    rest = slots[1:]
    any_ = pl.BlockSpec(memory_space=pl.ANY)

    def clip(v):
        return jnp.clip(v, 0, steps - 1)

    def layer(s):
        return LAYERS - 1 - s // per

    attend0 = (LAYERS - 1) * per + steps + 4
    img = lambda at: pl.BlockSpec((PAIR, SEQ, D), lambda s: (clip(s - at), 0, 0))
    mine = lambda at: pl.BlockSpec((PAIR, SEQ, D), lambda s: (lax.axis_index("mp") * steps + clip(s - at), 0, 0))
    wide = (COLS - ATT, ATT)
    part = rest[-1]
    if fast:
        outs = [
            jax.ShapeDtypeStruct((2, *rest, COLS - ATT), bf16),
            jax.ShapeDtypeStruct((2, LAYERS, part, FFH), f32), jax.ShapeDtypeStruct((1, part, COLS - ATT), f32),
        ]
        specs = [any_, whole(outs[1].shape), whole(outs[2].shape)]
        comm = Scatter.landing(part, FFH) * 2 + Scatter.landing(part, COLS - ATT)
        params = dict(collective_id=2, has_side_effects=True)
    else:
        outs = [
            jax.ShapeDtypeStruct((LAYERS, 2, *rest, COLS - ATT), bf16),
            jax.ShapeDtypeStruct((LAYERS, 2, 2, *rest, FFH), bf16),
        ]
        specs, comm, params = [any_, any_], [], {}
    small = [(LAYERS, 2, 2 * HALF), (LAYERS, 1, 2 * FFH), (LAYERS, GROUPS, WROW, LANES), (LAYERS, 8, D)]
    return pl.pallas_call(
        functools.partial(backward_kernel, fast, steps),
        name="backward",
        grid=(LAYERS * per,),
        in_specs=[
            mine(0), mine(attend0),
            pl.BlockSpec((ROWS, D), lambda s: (clip(s - steps - 4), 0)),
            pl.BlockSpec((ROWS, D), lambda s: (layer(s) * steps + clip(lax.rem(s, per)), 0)),
            pl.BlockSpec((WPAIR, 2 * QKV), lambda s: (layer(s) * steps + clip(lax.rem(s, per) - steps - 4), 0)),
            any_, any_, any_, any_, any_,
            *(whole(a.shape) for a in (bias, nv, perm, perm_t, hm)),
            pl.BlockSpec(memory_space=pltpu.SMEM),
        ],
        out_specs=[img(attend0), *specs, *(whole(n) for n in small)],
        out_shape=[
            jax.ShapeDtypeStruct((steps * PAIR, SEQ, D), f32), *outs, *(jax.ShapeDtypeStruct(n, f32) for n in small),
        ],
        scratch_shapes=[
            pltpu.VMEM((rows, D), f32), pltpu.VMEM((ROWS, D), f32),
            pltpu.VMEM((WPAIR, D), bf16), pltpu.VMEM((WPAIR, D), bf16), pltpu.VMEM((WPAIR, 2 * QKV), bf16),
            pltpu.VMEM((rows, 2 * FFH), bf16), pltpu.VMEM((rows, 2 * QKV), bf16),
            *[pltpu.VMEM((rows, D), bf16)] * 4,
            pltpu.VMEM((rows, 2 * FFH), bf16), pltpu.VMEM((rows, D), bf16),
            *(pltpu.VMEM((*slots, n), bf16) for n in wide),
            pltpu.VMEM((2, 2, *rest, FFH), bf16), pltpu.VMEM((2, *rest, COLS - ATT), bf16),
            *[pltpu.VMEM((SLOTS, WROW, LANES), f32)] * 2, *[pltpu.VMEM((SLOTS, WROW, LANES), bf16)] * 2,
            pltpu.SemaphoreType.DMA((8,)), *comm,
        ],
        compiler_params=pltpu.CompilerParams(vmem_limit_bytes=VLIM, **params),
    )(cot, tok, ys, mid, qkv, act, slope, mixed, wa, wm, bias, nv, perm, perm_t, hm, count)


def head_mask():
    return (np.arange(QUAD)[None, :] // HD == np.arange(GROUP)[:, None]).astype(np.float32)


def exact_parts(a):
    parts = []
    for _ in range(3):
        top = lax.reduce_precision(a, 8, 7)
        parts.append(top.astype(bf16))
        a = a - top
    return jnp.stack(parts)


def bias_cols(onehot, table):
    picked = jnp.einsum("jti,smlth->sjmlhi", onehot.astype(bf16), exact_parts(table), preferred_element_type=f32)
    picked = (picked[0] + picked[1] + picked[2]).transpose(1, 2, 0, 3, 4)
    picked = picked.reshape(-1, LAYERS, WROW, 2, GROUP, WROW).transpose(0, 1, 3, 2, 4, 5)
    apart = np.concatenate([np.zeros((1, WROW, WROW), np.float32), region_mask()])
    apart[:, WSEQ:] = pad_fill
    both = jnp.concatenate([picked[:, :1]] + [picked[:, 1:]] * 4, 1)
    both = (both + jnp.asarray(apart)[:, None, :, None, :]) * (1.0 / score_scale)
    return both.reshape(-1, 5, 2, WROW, LANES)

NZ, NY, NX = 4, 2, 2
PEERS = NZ * NY * NX
MESH_ID = pl.DeviceIdType.MESH


class Place:
    def __init__(self):
        d = lax.axis_index("dp")
        self.d, self.m = d, lax.axis_index("mp")
        self.z, self.y, self.x = d // 4, lax.rem(d // 2, 2), lax.rem(d, 2)

    def chip(self, z, y, x):
        return (z * NY + y) * NX + x

    def at(self, y=None, x=None, m=None):
        y = self.y if y is None else y
        x = self.x if x is None else x
        return (self.chip(self.z, y, x), self.m if m is None else m)

    def xn(self):
        return self.at(x=1 - self.x)

    def yn(self):
        return self.at(y=1 - self.y)

    def core(self):
        return self.at(m=1 - self.m)

    def zn(self, step):
        return (self.chip(self.z + step, self.y, self.x), self.m)

    def has(self, step):
        return self.z < NZ - 1 if step > 0 else self.z > 0

    def column(self, z):
        return (self.chip(z, self.y, self.x), self.m)


def remote(src, dst, send, recv, to):
    return pltpu.make_async_remote_copy(
        src_ref=src, dst_ref=dst, send_sem=send, recv_sem=recv, device_id=to, device_id_type=MESH_ID
    )


def neighbour_barrier(p):
    sem = pltpu.get_barrier_semaphore()
    partners = [p.xn(), p.yn(), p.core()] + [p.column(lax.rem(p.z + n, NZ)) for n in range(1, NZ)]
    for to in partners:
        pl.semaphore_signal(sem, inc=1, device_id=to, device_id_type=MESH_ID)
    pl.semaphore_wait(sem, len(partners))


def each_plane(body):
    lax.fori_loop(0, NZ, lambda k, carry: (body(k), carry)[1], 0)


class Gather:
    SEMS = 52
    BASE = {"z": 0, "xa": 8, "yb": 12, "ya0": 16, "ya1": 20, "xb0": 24, "xb1": 28,
            "own": 32, "ax": 36, "by": 40, "ar": 44, "br": 48}

    def __init__(self, own, full, send, recv, local):
        self.p, self.own, self.full = Place(), own, full
        self.send, self.recv, self.local = send, recv, local
        half = full.shape[-1] // 2
        self.all, self.a, self.b = pl.ds(0, 2 * half), pl.ds(0, half), pl.ds(half, half)

    def region(self, kind, k, arrived):
        p = self.p
        oy, ox = 1 - p.y, 1 - p.x
        if kind == "z":
            return (p.m, k, p.y, p.x), self.all, None
        if kind == "xa":
            return (p.m, k, p.y, ox if arrived else p.x), self.a, p.xn()
        if kind == "yb":
            return (p.m, k, oy if arrived else p.y, p.x), self.b, p.yn()
        if kind in ("ya0", "ya1"):
            return (p.m, k, oy if arrived else p.y, p.x if kind == "ya0" else ox), self.a, p.yn()
        if kind in ("xb0", "xb1"):
            return (p.m, k, p.y if kind == "xb0" else oy, ox if arrived else p.x), self.b, p.xn()
        m = 1 - p.m if arrived else p.m
        if kind == "own":
            return (m, k, p.y, p.x), self.all, p.core()
        if kind == "ax":
            return (m, k, p.y, ox), self.a, p.core()
        if kind == "by":
            return (m, k, oy, p.x), self.b, p.core()
        if kind == "ar":
            return (m, k, oy, slice(None)), self.a, p.core()
        return (m, k, slice(None), ox), self.b, p.core()

    def copy(self, kind, k, own=False, arrived=False, step=0):
        at, cols, to = self.region(kind, k, arrived)
        dst = self.full.at[(*at, slice(None), cols)]
        src = self.own.at[:, cols] if own else dst
        s = self.BASE[kind] + k
        r = s
        if kind == "z":
            to = self.p.zn(step)
            s = s + (4 if step < 0 else 0)
        return remote(src, dst, self.send.at[s], self.recv.at[r], to)

    def keep(self):
        p = self.p
        return pltpu.make_async_copy(
            self.own.at[:, self.all], self.full.at[p.m, p.z, p.y, p.x, :, self.all], self.local
        )

    def fan(self, k, own=False):
        for kind in ("xa", "yb", "ya0", "xb0", "own"):
            self.copy(kind, k, own).start()

    def stage(self, n):
        p = self.p
        if n == 0:
            self.keep().start()
            for step in (1, -1):
                pl.when(p.has(step))(lambda step=step: self.copy("z", p.z, True, step=step).start())
            self.fan(p.z, True)
        elif n <= 3:
            for step in (1, -1):
                k = p.z - step * n
                inside = k >= 0 if step > 0 else k < NZ

                @pl.when(inside)
                def _():
                    self.copy("z", k, arrived=True, step=step).wait_recv()
                    pl.when(p.has(step))(lambda: self.copy("z", k, step=step).start())
                    self.fan(k)
        elif n == 4:

            @each_plane
            def _(k):
                self.copy("xa", k, arrived=True).wait_recv()
                for kind in ("ya1", "ax"):
                    self.copy(kind, k).start()
                self.copy("yb", k, arrived=True).wait_recv()
                for kind in ("xb1", "by"):
                    self.copy(kind, k).start()
        elif n == 5:

            @each_plane
            def _(k):
                for kind, rest in (("ya", "ar"), ("xb", "br")):
                    for rel in ("0", "1"):
                        self.copy(kind + rel, k, arrived=True).wait_recv()
                    self.copy(rest, k).start()
        else:

            @each_plane
            def _(k):
                for kind in ("own", "ax", "by", "ar", "br"):
                    self.copy(kind, k, arrived=True).wait_recv()
                for kind in self.BASE:
                    if kind != "z":
                        self.copy(kind, k).wait_send()
                pl.when((k <= p.z) & p.has(1))(lambda: self.copy("z", k, step=1).wait_send())
                pl.when((k >= p.z) & p.has(-1))(lambda: self.copy("z", k, step=-1).wait_send())

            self.keep().wait()

    STAGES = 7


def add_into(ref, at, other):
    ref[at] = ref[at] + other


class Scatter:
    SEMS = 24
    BASE = {"core": 0, "ya": 4, "xb": 8, "xa": 12, "yb": 16, "z": 20}

    @staticmethod
    def landing(rows, cols):
        half = cols // 2
        return [
            pltpu.VMEM((NZ, NY, NX, rows, cols), bf16),
            pltpu.VMEM((NZ, NX, rows, half), bf16), pltpu.VMEM((NZ, NY, rows, half), bf16),
            pltpu.VMEM((NZ, rows, half), bf16), pltpu.VMEM((NZ, rows, half), bf16),
            pltpu.VMEM((NZ, rows, cols), bf16),
            pltpu.SemaphoreType.DMA((Scatter.SEMS,)), pltpu.SemaphoreType.DMA((Scatter.SEMS,)),
        ]

    def __init__(self, give, part, other, ya, xb, xa, yb, z, send, recv):
        self.p, self.give, self.part, self.other = Place(), give, part, other
        self.land = {"ya": ya, "xb": xb, "xa": xa, "yb": yb, "z": z}
        self.send, self.recv = send, recv
        half = part.shape[-1] // 2
        self.a, self.b = pl.ds(0, half), pl.ds(half, half)

    def copy(self, kind, k):
        p = self.p
        oy, ox = 1 - p.y, 1 - p.x
        full = slice(None)
        if kind == "core":
            src, dst, to = self.give.at[k], self.other.at[k], p.core()
        else:
            at, to = {
                "ya": ((k, oy, full, full, self.a), p.yn()),
                "xb": ((k, full, ox, full, self.b), p.xn()),
                "xa": ((k, p.y, ox, full, self.a), p.xn()),
                "yb": ((k, oy, p.x, full, self.b), p.yn()),
                "z": ((k, p.y, p.x, full, full), p.column(k)),
            }[kind]
            src, dst = self.part.at[at], self.land[kind].at[p.z if kind == "z" else k]
        s = self.BASE[kind] + k
        r = self.BASE[kind] + p.z if kind == "z" else s
        return remote(src, dst, self.send.at[s], self.recv.at[r], to)

    def landed(self, k):
        s = self.BASE["z"] + k
        at = self.land["z"].at[k]
        return remote(at, at, self.send.at[s], self.recv.at[s], self.p.column(k))

    def stage(self, n):
        p = self.p
        oy, ox = 1 - p.y, 1 - p.x
        if n == 0:
            each_plane(lambda k: self.copy("core", k).start())
        elif n == 1:

            @each_plane
            def _(k):
                self.copy("core", k).wait_recv()
                for y in range(NY):
                    for x in range(NX):
                        add_into(self.part, (k, y, x), self.other[k, y, x])
                self.copy("ya", k).start()
                self.copy("xb", k).start()
        elif n == 2:

            @each_plane
            def _(k):
                self.copy("ya", k).wait_recv()
                for x in range(NX):
                    add_into(self.part, (k, p.y, x, slice(None), self.a), self.land["ya"][k, x])
                self.copy("xa", k).start()
                self.copy("xb", k).wait_recv()
                for y in range(NY):
                    add_into(self.part, (k, y, p.x, slice(None), self.b), self.land["xb"][k, y])
                self.copy("yb", k).start()
        elif n == 3:

            @each_plane
            def _(k):
                self.copy("xa", k).wait_recv()
                add_into(self.part, (k, p.y, p.x, slice(None), self.a), self.land["xa"][k])
                self.copy("yb", k).wait_recv()
                add_into(self.part, (k, p.y, p.x, slice(None), self.b), self.land["yb"][k])

            for dist in (3, 2, 1):
                for k in (p.z + dist, p.z - dist):
                    pl.when((k >= 0) & (k < NZ))(lambda k=k: self.copy("z", k).start())
        else:

            @each_plane
            def _(k):
                for kind in ("core", "ya", "xb", "xa", "yb"):
                    self.copy(kind, k).wait_send()
                pl.when(k != p.z)(lambda: self.copy("z", k).wait_send())

    STAGES = 5

    def result(self, out):
        p = self.p
        out[...] = self.part[p.z, p.y, p.x].astype(f32)

        @each_plane
        def _(k):
            @pl.when(k != p.z)
            def _():
                self.landed(k).wait_recv()
                out[...] += self.land["z"][k].astype(f32)


class Total:
    STEPS = 5

    @staticmethod
    def scratch(shape):
        return [
            pltpu.VMEM((Total.STEPS, *shape), f32), pltpu.VMEM((Total.STEPS, *shape), f32),
            pltpu.SemaphoreType.DMA((Total.STEPS,)), pltpu.SemaphoreType.DMA((Total.STEPS,)),
        ]

    def __init__(self, start, held, land, send, recv):
        self.p, self.start, self.held, self.land, self.send, self.recv = Place(), start, held, land, send, recv

    def copy(self, n):
        p = self.p
        pair = p.z + 1 - 2 * lax.rem(p.z, 2)
        far = lax.rem(p.z + 2, NZ)
        to = (p.core(), p.yn(), p.xn(), (p.chip(pair, p.y, p.x), p.m), (p.chip(far, p.y, p.x), p.m))[n]
        src = self.start if n == 0 else self.held.at[n - 1]
        return remote(src, self.land.at[n], self.send.at[n], self.recv.at[n], to)

    def stage(self, n):
        if n > 0:
            self.copy(n - 1).wait_recv()
            before = self.start[...] if n == 1 else self.held[n - 2]
            self.held[n - 1] = before + self.land[n - 1]
        if n < self.STEPS:
            self.copy(n).start()
        else:
            for k in range(self.STEPS):
                self.copy(k).wait_send()


def tail_kernel(grad_ref, small_ref, out_ref, small_out, part, *refs):
    neighbour_barrier(Place())
    total = Total(small_ref, *refs[-4:])
    width = part.shape[-1]
    spans = [pl.ds(n * width, width) for n in range(2)]
    pieces = [
        Scatter(grad_ref.at[0, ..., cols], part.at[n], *refs[8 * n : 8 * n + 8]) for n, cols in enumerate(spans)
    ]
    for s in pieces:
        s.stage(0)
    total.stage(0)
    for n, cols in enumerate(spans):
        part[n] = grad_ref[1, ..., cols]
    for n in range(1, Scatter.STAGES - 1):
        for s in pieces:
            s.stage(n)
        total.stage(n)
    total.stage(Scatter.STAGES - 1)
    for s, cols in zip(pieces, spans):
        s.result(out_ref.at[:, cols])
        s.stage(Scatter.STAGES - 1)
    total.stage(Total.STEPS)
    small_out[...] = total.held[Total.STEPS - 1]


def tail(grad, small):
    rows, cols = grad.shape[-2:]
    half = cols // 2
    vm = pl.BlockSpec(memory_space=pltpu.VMEM)
    return pl.pallas_call(
        tail_kernel,
        name="tail",
        out_shape=[jax.ShapeDtypeStruct((rows, cols), f32), jax.ShapeDtypeStruct(small.shape, f32)],
        in_specs=[vm] * 2,
        out_specs=[vm] * 2,
        scratch_shapes=[pltpu.VMEM((2, *grad.shape[1:-1], half), bf16)] + Scatter.landing(rows, half) * 2
        + Total.scratch(small.shape),
        compiler_params=pltpu.CompilerParams(collective_id=3, has_side_effects=True, vmem_limit_bytes=VLIM),
    )(grad, small)


def adam_update(weight_in, moment_one, moment_two, grad_sum, decay):
    new_one = beta_one * moment_one + (1.0 - beta_one) * grad_sum
    new_two = beta_two * moment_two + (1.0 - beta_two) * grad_sum * grad_sum
    hat_one = new_one / (1.0 - beta_one**adam_step)
    hat_two = new_two / (1.0 - beta_two**adam_step)
    new_weight = weight_in - learn_rate * (hat_one / (jnp.sqrt(hat_two) + adam_eps) + decay * weight_in)
    return (new_weight, new_one, new_two)


def both_halves(mine, me):
    other = lax.ppermute(mine, "mp", [(0, 1), (1, 0)])
    low = jnp.where(me == 0, mine, other)
    high = jnp.where(me == 0, other, mine)
    return jnp.concatenate([low, high], 0)


HEADS = GROUPS * GROUP
LITTLE = 4 * HALF + 2 * FFH + HEADS * TABLE + 6 * D


def lanes_of(a):
    flat = a.reshape(-1)
    return jnp.pad(flat, (0, -flat.size % 1024)).reshape(-1, 128)


def sum_of_all(a):
    a = a.reshape(LAYERS, 2, D, a.shape[-1])
    total = a[:, 1].astype(f32) + lax.ppermute(a[:, 0], "mp", [(0, 1), (1, 0)]).astype(f32)
    return lax.psum_scatter(total.astype(bf16), "dp", scatter_dimension=1, tiled=True).astype(f32)


def pair_onehot(rel_index):
    index = jnp.pad(rel_index.T, ((0, WROW - WSEQ), (0, WROW - WSEQ)), constant_values=-1)
    return (index[:, None, :] == jnp.arange(TABLE, dtype=jnp.int32)[None, :, None]).astype(f32)


def local(
    fast, tokens, cotangent, image_count, rel_index,
    w_qkv, w_proj, w_fc_one, w_fc_two, qv_bias, fc_one_bias, rel_table, norm_vec,
    m_qkv, m_proj, m_fc_one, m_fc_two, m_qv_bias, m_fc_one_bias, m_rel_table, m_norm_vec,
    v_qkv, v_proj, v_fc_one, v_fc_two, v_qv_bias, v_fc_one_bias, v_rel_table, v_norm_vec,
):
    me = lax.axis_index("mp")
    images = tokens.shape[0]
    nimg = images // 2
    steps = nimg // PAIR
    part = w_qkv.shape[1]
    tok, cot = tokens, cotangent
    onehot = pair_onehot(rel_index)
    vecs = jnp.concatenate([fc_one_bias[:, None], jnp.pad(qv_bias, ((0, 0), (0, 5), (0, FFH - HALF)))], 1)
    shards = (w_qkv.transpose(0, 2, 1, 3), w_proj.transpose(0, 2, 1), w_fc_one, w_fc_two.transpose(0, 2, 1))
    if fast:
        bias = bias_cols(onehot, rel_table[None])[0]
    else:
        wm = jnp.concatenate([w_fc_one, w_fc_two.transpose(0, 2, 1)], 2).astype(bf16)
        wa = jnp.concatenate([w_qkv.reshape(LAYERS, part, QKV), w_proj.transpose(0, 2, 1)], 2).astype(bf16)
        shards = [
            lax.all_gather(w, ("mp", "dp")).reshape(2, -1, LAYERS, part, w.shape[-1]).transpose(2, 0, 1, 3, 4)
            .reshape(LAYERS, 2, 1, 1, 1, D, w.shape[-1])
            for w in (wa, wm)
        ]
        vecs = lax.all_gather(vecs, "mp")
        bias = bias_cols(onehot, lax.all_gather(rel_table, "mp"))
    hm = jnp.asarray(head_mask(), bf16)
    perms = np.stack([permutation(layer % 2 == 1) for layer in range(LAYERS)])
    perm, perm_t = jnp.asarray(perms, bf16), jnp.asarray(perms.transpose(0, 2, 1), bf16)
    out, *saved, all_wa, all_wm, bias = forward(
        tok, shards, bias, vecs, norm_vec, perm, perm_t, hm, fast, steps
    )
    weights = (all_wa, all_wm) if fast else shards
    out = both_halves(out, me)
    x_grad, *grads, gqv, gb1, ds, gnv = backward(
        cot, tok, saved, weights, bias, norm_vec, perm, perm_t, hm, image_count, fast, steps
    )
    x_grad = both_halves(x_grad, me)
    ds = ds.reshape(LAYERS, GROUPS, WROW, GROUP, WROW)
    gt = jnp.einsum("lgjhi,jti->lght", ds, onehot, precision=lax.Precision.HIGHEST)
    little = jnp.concatenate([a.reshape(LAYERS, -1) for a in (gqv, gb1, gt, gnv[:, :6])], 1)
    if fast:
        ga, sum_m, sum_a = grads
        last, total = tail(ga, lanes_of(little))
        big_a, big_m = jnp.stack([last, sum_a[0]]), sum_m
        little = total.reshape(-1)[: LAYERS * LITTLE].reshape(LAYERS, LITTLE)
    else:
        ga, gm = grads
        big_a, big_m = sum_of_all(ga), jnp.stack([sum_of_all(gm[:, n]) for n in range(2)])
        little = lax.psum(little, ("dp", "mp"))
    one_grad = big_m[0]
    two_grad = big_m[1].transpose(0, 2, 1)
    qkv_grad = big_a[:, :, :QKV].reshape(LAYERS, part, 3, HALF)
    proj_grad = big_a[:, :, QKV:].transpose(0, 2, 1)
    cut = lambda a: lax.dynamic_index_in_dim(a, me, 1, keepdims=False)
    at = 2 * 2 * HALF
    qv_grad = cut(little[:, :at].reshape(LAYERS, 2, 2, HALF).transpose(0, 2, 1, 3))
    bias_grad = cut(little[:, at : at + 2 * FFH].reshape(LAYERS, 2, FFH))
    at += 2 * FFH
    table_grad = cut(little[:, at : at + HEADS * TABLE].reshape(LAYERS, 2, HEADS // 2, TABLE)).transpose(0, 2, 1)
    at += HEADS * TABLE
    norm_grad = little[:, at:].reshape(LAYERS, 6, D)
    groups = [
        adam_update(w_qkv, m_qkv, v_qkv, qkv_grad, decay_rate),
        adam_update(w_proj, m_proj, v_proj, proj_grad, decay_rate),
        adam_update(w_fc_one, m_fc_one, v_fc_one, one_grad, decay_rate),
        adam_update(w_fc_two, m_fc_two, v_fc_two, two_grad, decay_rate),
        adam_update(qv_bias, m_qv_bias, v_qv_bias, qv_grad, 0.0),
        adam_update(fc_one_bias, m_fc_one_bias, v_fc_one_bias, bias_grad, 0.0),
        adam_update(rel_table, m_rel_table, v_rel_table, table_grad, 0.0),
        adam_update(norm_vec, m_norm_vec, v_norm_vec, norm_grad, 0.0),
    ]
    return (out, x_grad, *[grp[k] for k in range(3) for grp in groups])


def solution(mesh):
    params = (
        P(None, "dp", None, "mp"), P(None, "mp", "dp"), P(None, "dp", "mp"), P(None, "mp", "dp"),
        P(None, None, "mp"), P(None, "mp"), P(None, None, "mp"), P(),
    )
    act = (P("dp", None, None), P("dp", None, None))
    return jax.shard_map(
        functools.partial(local, mesh.shape["dp"] == PEERS),
        mesh=mesh,
        in_specs=(*act, P("dp"), P(), *params, *params, *params),
        out_specs=(*act, *params, *params, *params),
        check_vma=False,
    )
```

profile of v0, /device:TPU:0, one launch (start us, length us, event | category | flops | bytes accessed | tf_op | source)
XLA Modules:
  0.0 272.3 jit_solution(4993151944208428479)
XLA Ops:
  0.7 0.7 fusion.35
  1.4 0.8 copy.99
  2.2 1.2 fusion.8
  3.4 0.0 copy-start.13
  3.4 0.1 slice_add_fusion
  3.5 0.0 copy-start.14
  3.5 0.0 copy-start.20
  3.6 0.1 copy.113
  3.7 0.3 concatenate.23
  4.0 0.2 concatenate.24
  4.2 0.1 copy-done.13
  4.3 0.1 add.178
  4.5 0.4 add.179
  4.9 0.6 copy.87.refs_6_.nv_ref
  6.2 0.6 select_maximum_fusion.refs_5_
  6.8 0.9 fusion.14.refs_4_
  7.7 101.8 %forward.1 = (f32[6,196,512]{2,1,0:T(8,128)}, f32[1200,512]{1,0:T(8,128)}, f32[2400,512]{1,0:T(8,128)}, bf16[3072,1536]{1,0:T(8,128)(2,1)}, bf16[2400,512]{1,0:T...) custom-call(bf16[12,196,512]{2,1,0:T(8,128)(2,1)} %tok_ref.3, ...), custom_call_target="tpu_custom_call" | custom-call | tf_op jit(solution)/shard_map/forward/pallas_call | solution.py:631
  109.5 103.0 %backward.1 = (f32[6,196,512]{2,1,0:T(8,128)}, bf16[2,4,2,2,32,1024]{5,4,3,2,1,0:T(8,128)(2,1)}, f32[2,2,32,1024]{3,2,1,0:T(8,128)}, f32[1,32,1024]{2,1,0:T(8,12...) custom-call(f32[12,196,512]{2,1,0:T(8,128)} %cot_ref.1, ...), custom_call_target="tpu_custom_call" | custom-call | tf_op jit(solution)/shard_map/backward/pallas_call | solution.py:708
  212.5 0.1 collective-permute-start.1
  212.6 0.5 collective-permute-start
  213.1 1.5 reshape.179
  214.6 0.0 copy-start.19
  214.6 1.7 fusion.11
  216.3 0.0 copy-start.7
  216.3 0.0 copy-start.15
  216.4 0.1 reshape.180
  216.6 0.1 concatenate.29
  216.7 0.1 reshape.182
  216.8 0.6 pad_bitcast_fusion.small_ref
  217.5 31.0 %tail.1 = (f32[32,1024]{1,0:T(8,128)}, f32[144,128]{1,0:T(8,128)}) custom-call(bf16[2,4,2,2,32,1024]{5,4,3,2,1,0:T(8,128)(2,1)} %get-tuple-element.57.grad_ref, f32[144,128]{1,0:T(8,128)} %pad_bitcast_fusion.small_ref), custom_call_target="tpu_custom_call" | custom-call | tf_op jit(solution)/shard_map/tail/pallas_call | solution.py:1100
  248.5 1.0 reshape.186
  249.5 0.0 copy-start.3
  249.5 0.0 copy-start.10
  249.5 0.1 slice.68
  249.7 0.1 reshape.189
  249.8 0.9 fusion.19
  250.7 1.4 multiply_subtract_fusion.6
  252.1 1.3 multiply_subtract_fusion.7
  253.4 1.4 multiply_subtract_fusion.5
  254.8 1.4 multiply_subtract_fusion.4
  256.3 1.5 multiply_subtract_fusion.3
  257.8 2.0 multiply_subtract_fusion.2
  259.8 1.0 multiply_subtract_fusion
  260.8 1.0 multiply_subtract_fusion.1
  261.8 2.3 broadcast_select_fusion.1
  264.1 2.8 %pad_maximum_fusion.1 = f32[12,196,512]{2,1,0:T(8,128)} fusion(f32[6,196,512]{2,1,0:T(8,128)S(1)} %get-tuple-element.117, f32[6,196,512]{2,1,0:T(8,128)S(1)} %get-tuple-element.116), kind=kLoop, calls=%fused_computation.1 | loop fusion | flops 1204224 | bytes 9633792 | tf_op jit(solution)/shard_map/concatenate | solution.py:1125
  267.0 2.6 broadcast_select_fusion.3
  269.5 2.8 %pad_maximum_fusion = f32[12,196,512]{2,1,0:T(8,128)} fusion(f32[6,196,512]{2,1,0:T(8,128)S(1)} %get-tuple-element.119, f32[6,196,512]{2,1,0:T(8,128)S(1)} %get-tuple-element.118), kind=kLoop, calls=%fused_computation | loop fusion | flops 1204224 | bytes 9633792 | tf_op jit(solution)/shard_map/concatenate | solution.py:1125
  (51 shorter events, 0.2 us)
Async XLA Ops:
  3.4 0.9 copy-start.13
  3.5 1.3 copy-start.14
  3.5 2.0 copy-start.17
  3.5 2.6 copy-start.20
  212.5 4.0 %copy-start.18 = (f32[2,8,512]{2,1,0:T(8,128)S(1)}, f32[2,8,512]{2,1,0:T(8,128)}, u32[]{:S(2)}) copy-start(f32[2,8,512]{2,1,0:T(8,128)} %get-tuple-element.61) | copy-start | bytes 98308
  212.5 4.0 %copy-start.21 = (f32[2,1,2048]{2,1,0:T(1,128)S(1)}, f32[2,1,2048]{2,1,0:T(1,128)}, u32[]{:S(2)}) copy-start(f32[2,1,2048]{2,1,0:T(1,128)} %get-tuple-element.59) | copy-start | bytes 49156
  212.5 4.0 %copy-start.22 = (f32[2,2,512]{2,1,0:T(2,128)S(1)}, f32[2,2,512]{2,1,0:T(2,128)}, u32[]{:S(2)}) copy-start(f32[2,2,512]{2,1,0:T(2,128)} %get-tuple-element.58) | copy-start | bytes 24580
  212.5 49.3 %collective-permute-start.1 = (f32[6,196,512]{2,1,0:T(8,128)}, f32[6,196,512]{2,1,0:T(8,128)}, u32[]{:S(2)}, u32[]{:S(2)}) collective-permute-start(f32[6,196,512]{2,1,0:T(8,128)} %get-tuple-element.56), channel_id=1, source_target_pairs={{0,1},{1,0},{2,3},{3,2},{4,5},{5,4},{6,7},{7,6},{8,9},{9,8},{10,11... | collective-permute-start | bytes 7225352 | tf_op jit(solution)/shard_map/ppermute | solution.py:1122
  212.6 54.4 %collective-permute-start = (f32[6,196,512]{2,1,0:T(8,128)}, f32[6,196,512]{2,1,0:T(8,128)}, u32[]{:S(2)}, u32[]{:S(2)}) collective-permute-start(f32[6,196,512]{2,1,0:T(8,128)} %get-tuple-element.46), channel_id=1, source_target_pairs={{0,1},{1,0},{2,3},{3,2},{4,5},{5,4},{6,7},{7,6},{8,9},{9,8},{10,11... | collective-permute-start | bytes 7225352 | tf_op jit(solution)/shard_map/ppermute | solution.py:1122
  214.6 35.2 %copy-start.6 = (f32[1,32,1024]{2,1,0:T(8,128)S(1)}, f32[1,32,1024]{2,1,0:T(8,128)}, u32[]{:S(2)}) copy-start(f32[1,32,1024]{2,1,0:T(8,128)} %get-tuple-element.63) | copy-start | bytes 393220
  214.6 38.8 %copy-start.16 = (f32[2,169,8]{1,2,0:T(8,128)S(1)}, f32[2,169,8]{1,2,0:T(8,128)}, u32[]{:S(2)}) copy-start(f32[2,169,8]{1,2,0:T(8,128)} %param.42) | copy-start | bytes 32452
  214.6 40.2 %copy-start.19 = (f32[2,6,512]{2,0,1:T(2,128)S(1)}, f32[2,6,512]{2,0,1:T(2,128)}, u32[]{:S(2)}) copy-start(f32[2,6,512]{2,0,1:T(2,128)} %param.51) | copy-start | bytes 73732
  216.3 40.0 %copy-start.7 = (f32[2,256,32]{1,2,0:T(8,128)S(1)}, f32[2,256,32]{1,2,0:T(8,128)}, u32[]{:S(2)}) copy-start(f32[2,256,32]{1,2,0:T(8,128)} %param.37) | copy-start | bytes 196612
  216.3 39.9 %copy-start.15 = (f32[2,256,32]{1,2,0:T(8,128)S(1)}, f32[2,256,32]{1,2,0:T(8,128)}, u32[]{:S(2)}) copy-start(f32[2,256,32]{1,2,0:T(8,128)} %param.45) | copy-start | bytes 196612
  216.3 41.5 %copy-start.4 = (f32[2,32,3,256]{3,1,2,0:T(8,128)S(1)}, f32[2,32,3,256]{3,1,2,0:T(8,128)}, u32[]{:S(2)}) copy-start(f32[2,32,3,256]{3,1,2,0:T(8,128)} %param.36) | copy-start | bytes 589828
  216.3 41.5 %copy-start.12 = (f32[2,32,3,256]{3,1,2,0:T(8,128)S(1)}, f32[2,32,3,256]{3,1,2,0:T(8,128)}, u32[]{:S(2)}) copy-start(f32[2,32,3,256]{3,1,2,0:T(8,128)} %param.44) | copy-start | bytes 589828
  217.5 42.3 %copy-start.2 = (f32[2,1024,32]{1,2,0:T(8,128)S(1)}, f32[2,1024,32]{1,2,0:T(8,128)}, u32[]{:S(2)}) copy-start(f32[2,1024,32]{1,2,0:T(8,128)} %param.39) | copy-start | bytes 786436
  217.5 42.3 %copy-start.5 = (f32[2,2,32,1024]{3,2,1,0:T(8,128)S(1)}, f32[2,2,32,1024]{3,2,1,0:T(8,128)}, u32[]{:S(2)}) copy-start(f32[2,2,32,1024]{3,2,1,0:T(8,128)} %get-tuple-element.64) | copy-start | bytes 1572868
  217.5 42.3 %copy-start.8 = (f32[2,1024,32]{1,2,0:T(8,128)S(1)}, f32[2,1024,32]{1,2,0:T(8,128)}, u32[]{:S(2)}) copy-start(f32[2,1024,32]{1,2,0:T(8,128)} %param.47) | copy-start | bytes 786436
  217.5 42.3 %copy-start.9 = (f32[2,1024,32]{1,2,0:T(8,128)S(1)}, f32[2,1024,32]{1,2,0:T(8,128)}, u32[]{:S(2)}) copy-start(f32[2,1024,32]{1,2,0:T(8,128)} %param.55) | copy-start | bytes 786436
  249.5 11.3 %copy-start.3 = (f32[2,32,1024]{2,1,0:T(8,128)S(1)}, f32[2,32,1024]{2,1,0:T(8,128)}, u32[]{:S(2)}) copy-start(f32[2,32,1024]{2,1,0:T(8,128)} %refs_2_.1) | copy-start | bytes 786436
  249.5 11.3 %copy-start.10 = (f32[2,32,1024]{2,1,0:T(8,128)S(1)}, f32[2,32,1024]{2,1,0:T(8,128)}, u32[]{:S(2)}) copy-start(f32[2,32,1024]{2,1,0:T(8,128)} %param.46) | copy-start | bytes 786436
  249.5 11.3 %copy-start.11 = (f32[2,32,1024]{2,1,0:T(8,128)S(1)}, f32[2,32,1024]{2,1,0:T(8,128)}, u32[]{:S(2)}) copy-start(f32[2,32,1024]{2,1,0:T(8,128)} %param.54) | copy-start | bytes 786436
  257.8 4.0 %copy-start.1 = (f32[6,196,512]{2,1,0:T(8,128)S(1)}, f32[6,196,512]{2,1,0:T(8,128)}, u32[]{:S(2)}) copy-start(f32[6,196,512]{2,1,0:T(8,128)} %get-tuple-element.56) | copy-start | bytes 7225348
  264.1 2.8 %copy-start = (f32[6,196,512]{2,1,0:T(8,128)S(1)}, f32[6,196,512]{2,1,0:T(8,128)}, u32[]{:S(2)}) copy-start(f32[6,196,512]{2,1,0:T(8,128)} %get-tuple-element.46) | copy-start | bytes 7225348
where the time goes:
time: 273 us; the launch traced here: 272 us
  Pallas kernels  236 us (86%)
  other arithmetic  24.8 us (9%)
  local copies, waits for them, and re-layouts  6.63 us (2%)
  matrix products  2.86 us (1%)
    pallas_call x1, Pallas kernels, backward(): pl.pallas_call(functools.partial(backward_kernel, fast, steps), name='bac...  103 us
    pallas_call x1, Pallas kernels, forward(): pl.pallas_call(functools.partial(forward_kernel, fast, steps), name='forw...  102 us
    pallas_call x1, Pallas kernels, tail(): pl.pallas_call(tail_kernel, name='tail', out_shape=[jax.ShapeDtypeStruct(...  31 us
    sub x8, other arithmetic, adam_update(): weight_in - learn_rate * (hat_one / (jnp.sqrt(hat_two) + adam_eps) + deca...  11 us
    concatenate x2, other arithmetic, both_halves(): return jnp.concatenate([low, high], 0)  5.61 us
  transfers between devices with their start and end apart: 2, of which 0 were waited for; matrix products, arithmetic and copies ran while one was open for 8% of the time, Pallas kernels for 11%

commit v1 on v0

--- a/solution.py
+++ b/solution.py
@@ -408,23 +408,7 @@
         own_m[l, :, FFH:] = w_two[l].astype(bf16)
 
 
-FORWARD_PLAN = {
-    (0, 0): [(0, 0), (1, 0), (0, 1), (0, 2), (0, 3), (1, 1), (0, 4), (1, 2), (1, 3), (0, 5), (0, 6)],
-    (1, 1): [(1, 4)],
-    (2, 1): [(1, 5)],
-    (3, 0): [(2, 0), (1, 6)],
-    (3, 2): [(2, 1)],
-    (4, 0): [(2, 2)],
-    (4, 1): [(2, 3), (3, 0)],
-    (4, 3): [(2, 4)],
-    (5, 0): [(3, 1)],
-    (5, 1): [(2, 5), (3, 2)],
-    (6, 0): [(2, 6)],
-    (6, 1): [(3, 3)],
-    (7, 1): [(3, 4)],
-    (8, 1): [(3, 5)],
-    (9, 0): [(3, 6)],
-}
+FORWARD_PLAN = {(0, 0): [(0, 0), (1, 0), (0, 1), (0, 2), (0, 3), (1, 1), (0, 4), (1, 2), (1, 3), (0, 5), (0, 6), (2, 0)], (1, 1): [(1, 4), (3, 0)], (2, 1): [(1, 5), (2, 1)], (2, 2): [(2, 2), (2, 3)], (3, 0): [(1, 6)], (3, 2): [(2, 4), (3, 1)], (4, 0): [(3, 2)], (4, 2): [(2, 5), (3, 3)], (5, 2): [(2, 6)], (6, 1): [(3, 4)], (7, 4): [(3, 5)], (9, 0): [(3, 6)]}
 
 
 def backward_kernel(fast, steps, cot_ref, tok_ref, ys_ref, mid_ref, qkv_ref, act_in, slope_in, mixed_in, wa_in, wm_in,
@@ -573,32 +557,7 @@
         pl.when(r == per - 1)(lambda: flush(gwa, ga_out.at[layer]))
 
 
-BACKWARD_PLAN = {
-    (4, 0): [(0, 0)],
-    (5, 0): [(0, 1)],
-    (6, 0): [(1, 0)],
-    (7, 0): [(1, 1)],
-    (7, 4): [(0, 2)],
-    (8, 1): [(0, 3)],
-    (8, 2): [(1, 2)],
-    (9, 4): [(1, 3)],
-    (10, 0): [(0, 4)],
-    (11, 0): [(2, 0)],
-    (12, 0): [(2, 1)],
-    (13, 0): [(1, 4)],
-    (13, 3): [(2, 2)],
-    (14, 3): [(2, 3)],
-    (16, 0): [(0, 0)],
-    (17, 0): [(2, 4), (0, 1)],
-    (18, 0): [(1, 0)],
-    (19, 0): [(1, 1)],
-    (19, 4): [(0, 2)],
-    (20, 1): [(0, 3)],
-    (20, 2): [(1, 2)],
-    (21, 4): [(1, 3)],
-    (22, 0): [(0, 4)],
-    (23, 1): [(1, 4)],
-}
+BACKWARD_PLAN = {(4, 0): [(0, 0)], (5, 1): [(0, 1)], (6, 0): [(1, 0)], (7, 1): [(1, 1)], (7, 2): [(0, 2)], (8, 4): [(0, 3)], (8, 2): [(1, 2)], (9, 2): [(1, 3)], (10, 1): [(0, 4)], (11, 0): [(2, 0)], (12, 1): [(2, 1)], (13, 1): [(1, 4)], (14, 0): [(2, 2)], (15, 0): [(2, 3)], (16, 0): [(0, 0)], (17, 0): [(2, 4)], (17, 1): [(0, 1)], (18, 0): [(1, 0)], (19, 1): [(1, 1)], (19, 2): [(0, 2)], (20, 4): [(0, 3)], (20, 2): [(1, 2)], (21, 2): [(1, 3)], (22, 1): [(0, 4)], (23, 1): [(1, 4)]}
 
 
 def whole(shape, buffers=1):
@@ -788,12 +747,6 @@
     def core(self):
         return self.at(m=1 - self.m)
 
-    def zn(self, step):
-        return (self.chip(self.z + step, self.y, self.x), self.m)
-
-    def has(self, step):
-        return self.z < NZ - 1 if step > 0 else self.z > 0
-
     def column(self, z):
         return (self.chip(z, self.y, self.x), self.m)
 
@@ -817,9 +770,9 @@
 
 
 class Gather:
-    SEMS = 52
-    BASE = {"z": 0, "xa": 8, "yb": 12, "ya0": 16, "ya1": 20, "xb0": 24, "xb1": 28,
-            "own": 32, "ax": 36, "by": 40, "ar": 44, "br": 48}
+    SEMS = 48
+    BASE = {"z": 0, "xa": 4, "yb": 8, "ya0": 12, "ya1": 16, "xb0": 20, "xb1": 24,
+            "own": 28, "ax": 32, "by": 36, "ar": 40, "br": 44}
 
     def __init__(self, own, full, send, recv, local):
         self.p, self.own, self.full = Place(), own, full
@@ -831,7 +784,7 @@
         p = self.p
         oy, ox = 1 - p.y, 1 - p.x
         if kind == "z":
-            return (p.m, k, p.y, p.x), self.all, None
+            return (p.m, k if arrived else p.z, p.y, p.x), self.all, p.column(k)
         if kind == "xa":
             return (p.m, k, p.y, ox if arrived else p.x), self.a, p.xn()
         if kind == "yb":
@@ -851,15 +804,12 @@
             return (m, k, oy, slice(None)), self.a, p.core()
         return (m, k, slice(None), ox), self.b, p.core()
 
-    def copy(self, kind, k, own=False, arrived=False, step=0):
+    def copy(self, kind, k, own=False, arrived=False):
         at, cols, to = self.region(kind, k, arrived)
         dst = self.full.at[(*at, slice(None), cols)]
         src = self.own.at[:, cols] if own else dst
         s = self.BASE[kind] + k
-        r = s
-        if kind == "z":
-            to = self.p.zn(step)
-            s = s + (4 if step < 0 else 0)
+        r = self.p.z if kind == "z" and not arrived else s
         return remote(src, dst, self.send.at[s], self.recv.at[r], to)
 
     def keep(self):
@@ -876,18 +826,16 @@
         p = self.p
         if n == 0:
             self.keep().start()
-            for step in (1, -1):
-                pl.when(p.has(step))(lambda step=step: self.copy("z", p.z, True, step=step).start())
+            for dist in (1, 2, 3):
+                for k in (p.z + dist, p.z - dist):
+                    pl.when((k >= 0) & (k < NZ))(lambda k=k: self.copy("z", k, True).start())
             self.fan(p.z, True)
         elif n <= 3:
-            for step in (1, -1):
-                k = p.z - step * n
-                inside = k >= 0 if step > 0 else k < NZ
-
-                @pl.when(inside)
+            for k in (p.z + n, p.z - n):
+
+                @pl.when((k >= 0) & (k < NZ))
                 def _():
-                    self.copy("z", k, arrived=True, step=step).wait_recv()
-                    pl.when(p.has(step))(lambda: self.copy("z", k, step=step).start())
+                    self.copy("z", k, arrived=True).wait_recv()
                     self.fan(k)
         elif n == 4:
 
@@ -916,8 +864,7 @@
                 for kind in self.BASE:
                     if kind != "z":
                         self.copy(kind, k).wait_send()
-                pl.when((k <= p.z) & p.has(1))(lambda: self.copy("z", k, step=1).wait_send())
-                pl.when((k >= p.z) & p.has(-1))(lambda: self.copy("z", k, step=-1).wait_send())
+                pl.when(k != p.z)(lambda: self.copy("z", k, True).wait_send())
 
             self.keep().wait()
 

time: 273 us -> 262 us (0.960)
  Pallas kernels: 236 us -> 225 us
    pallas_call x1, Pallas kernels: 102 us -> 90.7 us  [forward(): pl.pallas_call(functools.partial(forward_kernel, fast, steps), name='forw...]
  transfers between devices with their start and end apart: 2 -> 2, of which waited for: 0 -> 0; matrix products, arithmetic and copies ran while one was open for 8% -> 9% of each run, Pallas kernels for 11% -> 11%
where the time goes in v1:
time: 262 us
  Pallas kernels  225 us (86%)
  other arithmetic  24.8 us (9%)
  local copies, waits for them, and re-layouts  6.63 us (3%)
  matrix products  2.86 us (1%)
    pallas_call x1, Pallas kernels, backward(): pl.pallas_call(functools.partial(backward_kernel, fast, steps), name='bac...  105 us
    pallas_call x1, Pallas kernels, forward(): pl.pallas_call(functools.partial(forward_kernel, fast, steps), name='forw...  90.7 us
    pallas_call x1, Pallas kernels, tail(): pl.pallas_call(tail_kernel, name='tail', out_shape=[jax.ShapeDtypeStruct(...  29.2 us
    sub x8, other arithmetic, adam_update(): weight_in - learn_rate * (hat_one / (jnp.sqrt(hat_two) + adam_eps) + deca...  11 us
    concatenate x2, other arithmetic, both_halves(): return jnp.concatenate([low, high], 0)  5.61 us
  transfers between devices with their start and end apart: 2, of which 0 were waited for; matrix products, arithmetic and copies ran while one was open for 9% of the time, Pallas kernels for 11%

profile of v1, /device:TPU:0, one launch (start us, length us, event | category | flops | bytes accessed | tf_op | source)
XLA Modules:
  0.0 261.5 jit_solution(14114445268958235543)
XLA Ops:
  0.7 0.7 fusion.35
  1.4 0.8 copy.99
  2.2 1.2 fusion.8
  3.4 0.0 copy-start.13
  3.4 0.1 slice_add_fusion
  3.5 0.0 copy-start.14
  3.5 0.0 copy-start.20
  3.6 0.1 copy.113
  3.7 0.3 concatenate.23
  4.0 0.2 concatenate.24
  4.2 0.1 copy-done.13
  4.3 0.1 add.178
  4.5 0.4 add.179
  4.9 0.6 copy.87.refs_6_.nv_ref
  6.2 0.6 select_maximum_fusion.refs_5_
  6.8 0.9 fusion.14.refs_4_
  7.7 90.7 %forward.1 = (f32[6,196,512]{2,1,0:T(8,128)}, f32[1200,512]{1,0:T(8,128)}, f32[2400,512]{1,0:T(8,128)}, bf16[3072,1536]{1,0:T(8,128)(2,1)}, bf16[2400,512]{1,0:T...) custom-call(bf16[12,196,512]{2,1,0:T(8,128)(2,1)} %tok_ref.3, ...), custom_call_target="tpu_custom_call" | custom-call | tf_op jit(solution)/shard_map/forward/pallas_call | solution.py:590
  98.4 105.1 %backward.1 = (f32[6,196,512]{2,1,0:T(8,128)}, bf16[2,4,2,2,32,1024]{5,4,3,2,1,0:T(8,128)(2,1)}, f32[2,2,32,1024]{3,2,1,0:T(8,128)}, f32[1,32,1024]{2,1,0:T(8,12...) custom-call(f32[12,196,512]{2,1,0:T(8,128)} %cot_ref.1, ...), custom_call_target="tpu_custom_call" | custom-call | tf_op jit(solution)/shard_map/backward/pallas_call | solution.py:667
  203.5 0.1 collective-permute-start.1
  203.6 0.5 collective-permute-start
  204.1 1.5 reshape.179
  205.6 0.0 copy-start.16
  205.6 1.7 fusion.11
  207.3 0.0 copy-start.15
  207.3 0.0 copy-start.4
  207.4 0.1 reshape.180
  207.6 0.1 concatenate.29
  207.7 0.1 reshape.182
  207.8 0.6 pad_bitcast_fusion.small_ref
  208.5 29.2 %tail.1 = (f32[32,1024]{1,0:T(8,128)}, f32[144,128]{1,0:T(8,128)}) custom-call(bf16[2,4,2,2,32,1024]{5,4,3,2,1,0:T(8,128)(2,1)} %get-tuple-element.57.grad_ref, f32[144,128]{1,0:T(8,128)} %pad_bitcast_fusion.small_ref), custom_call_target="tpu_custom_call" | custom-call | tf_op jit(solution)/shard_map/tail/pallas_call | solution.py:1047
  237.7 1.0 reshape.186
  238.7 0.0 copy-start.3
  238.7 0.0 copy-start.11
  238.7 0.1 slice.68
  238.9 0.1 reshape.189
  239.0 0.9 fusion.19
  239.9 1.4 multiply_subtract_fusion.6
  241.3 1.3 multiply_subtract_fusion.7
  242.6 1.4 multiply_subtract_fusion.5
  244.0 1.4 multiply_subtract_fusion.4
  245.5 1.5 multiply_subtract_fusion.3
  247.0 2.0 multiply_subtract_fusion.2
  249.0 1.0 multiply_subtract_fusion
  250.0 1.0 multiply_subtract_fusion.1
  251.0 2.3 broadcast_select_fusion.1
  253.3 2.8 %pad_maximum_fusion.1 = f32[12,196,512]{2,1,0:T(8,128)} fusion(f32[6,196,512]{2,1,0:T(8,128)S(1)} %get-tuple-element.117, f32[6,196,512]{2,1,0:T(8,128)S(1)} %get-tuple-element.116), kind=kLoop, calls=%fused_computation.1 | loop fusion | flops 1204224 | bytes 9633792 | tf_op jit(solution)/shard_map/concatenate | solution.py:1072
  256.2 2.6 broadcast_select_fusion.3
  258.7 2.8 %pad_maximum_fusion = f32[12,196,512]{2,1,0:T(8,128)} fusion(f32[6,196,512]{2,1,0:T(8,128)S(1)} %get-tuple-element.119, f32[6,196,512]{2,1,0:T(8,128)S(1)} %get-tuple-element.118), kind=kLoop, calls=%fused_computation | loop fusion | flops 1204224 | bytes 9633792 | tf_op jit(solution)/shard_map/concatenate | solution.py:1072
  (51 shorter events, 0.2 us)
Async XLA Ops:
  3.4 0.9 copy-start.13
  3.5 1.3 copy-start.14
  3.5 2.0 copy-start.17
  3.5 2.6 copy-start.20
  203.5 4.0 %copy-start.18 = (f32[2,8,512]{2,1,0:T(8,128)S(1)}, f32[2,8,512]{2,1,0:T(8,128)}, u32[]{:S(2)}) copy-start(f32[2,8,512]{2,1,0:T(8,128)} %get-tuple-element.61) | copy-start | bytes 98308
  203.5 4.0 %copy-start.21 = (f32[2,1,2048]{2,1,0:T(1,128)S(1)}, f32[2,1,2048]{2,1,0:T(1,128)}, u32[]{:S(2)}) copy-start(f32[2,1,2048]{2,1,0:T(1,128)} %get-tuple-element.59) | copy-start | bytes 49156
  203.5 4.0 %copy-start.22 = (f32[2,2,512]{2,1,0:T(2,128)S(1)}, f32[2,2,512]{2,1,0:T(2,128)}, u32[]{:S(2)}) copy-start(f32[2,2,512]{2,1,0:T(2,128)} %get-tuple-element.58) | copy-start | bytes 24580
  203.5 47.5 %collective-permute-start.1 = (f32[6,196,512]{2,1,0:T(8,128)}, f32[6,196,512]{2,1,0:T(8,128)}, u32[]{:S(2)}, u32[]{:S(2)}) collective-permute-start(f32[6,196,512]{2,1,0:T(8,128)} %get-tuple-element.56), channel_id=1, source_target_pairs={{0,1},{1,0},{2,3},{3,2},{4,5},{5,4},{6,7},{7,6},{8,9},{9,8},{10,11... | collective-permute-start | bytes 7225352 | tf_op jit(solution)/shard_map/ppermute | solution.py:1069
  203.6 52.5 %collective-permute-start = (f32[6,196,512]{2,1,0:T(8,128)}, f32[6,196,512]{2,1,0:T(8,128)}, u32[]{:S(2)}, u32[]{:S(2)}) collective-permute-start(f32[6,196,512]{2,1,0:T(8,128)} %get-tuple-element.46), channel_id=1, source_target_pairs={{0,1},{1,0},{2,3},{3,2},{4,5},{5,4},{6,7},{7,6},{8,9},{9,8},{10,11... | collective-permute-start | bytes 7225352 | tf_op jit(solution)/shard_map/ppermute | solution.py:1069
  205.6 33.4 %copy-start.6 = (f32[1,32,1024]{2,1,0:T(8,128)S(1)}, f32[1,32,1024]{2,1,0:T(8,128)}, u32[]{:S(2)}) copy-start(f32[1,32,1024]{2,1,0:T(8,128)} %get-tuple-element.63) | copy-start | bytes 393220
  205.6 37.0 %copy-start.16 = (f32[2,169,8]{1,2,0:T(8,128)S(1)}, f32[2,169,8]{1,2,0:T(8,128)}, u32[]{:S(2)}) copy-start(f32[2,169,8]{1,2,0:T(8,128)} %param.42) | copy-start | bytes 32452
  205.6 38.4 %copy-start.19 = (f32[2,6,512]{2,0,1:T(2,128)S(1)}, f32[2,6,512]{2,0,1:T(2,128)}, u32[]{:S(2)}) copy-start(f32[2,6,512]{2,0,1:T(2,128)} %param.51) | copy-start | bytes 73732
  207.3 38.1 %copy-start.7 = (f32[2,256,32]{1,2,0:T(8,128)S(1)}, f32[2,256,32]{1,2,0:T(8,128)}, u32[]{:S(2)}) copy-start(f32[2,256,32]{1,2,0:T(8,128)} %param.37) | copy-start | bytes 196612
  207.3 38.1 %copy-start.15 = (f32[2,256,32]{1,2,0:T(8,128)S(1)}, f32[2,256,32]{1,2,0:T(8,128)}, u32[]{:S(2)}) copy-start(f32[2,256,32]{1,2,0:T(8,128)} %param.45) | copy-start | bytes 196612
  207.3 39.7 %copy-start.4 = (f32[2,32,3,256]{3,1,2,0:T(8,128)S(1)}, f32[2,32,3,256]{3,1,2,0:T(8,128)}, u32[]{:S(2)}) copy-start(f32[2,32,3,256]{3,1,2,0:T(8,128)} %param.36) | copy-start | bytes 589828
  207.3 39.7 %copy-start.12 = (f32[2,32,3,256]{3,1,2,0:T(8,128)S(1)}, f32[2,32,3,256]{3,1,2,0:T(8,128)}, u32[]{:S(2)}) copy-start(f32[2,32,3,256]{3,1,2,0:T(8,128)} %param.44) | copy-start | bytes 589828
  208.5 40.5 %copy-start.2 = (f32[2,1024,32]{1,2,0:T(8,128)S(1)}, f32[2,1024,32]{1,2,0:T(8,128)}, u32[]{:S(2)}) copy-start(f32[2,1024,32]{1,2,0:T(8,128)} %param.39) | copy-start | bytes 786436
  208.5 40.5 %copy-start.5 = (f32[2,2,32,1024]{3,2,1,0:T(8,128)S(1)}, f32[2,2,32,1024]{3,2,1,0:T(8,128)}, u32[]{:S(2)}) copy-start(f32[2,2,32,1024]{3,2,1,0:T(8,128)} %get-tuple-element.64) | copy-start | bytes 1572868
  208.5 40.5 %copy-start.8 = (f32[2,1024,32]{1,2,0:T(8,128)S(1)}, f32[2,1024,32]{1,2,0:T(8,128)}, u32[]{:S(2)}) copy-start(f32[2,1024,32]{1,2,0:T(8,128)} %param.47) | copy-start | bytes 786436
  208.5 40.5 %copy-start.9 = (f32[2,1024,32]{1,2,0:T(8,128)S(1)}, f32[2,1024,32]{1,2,0:T(8,128)}, u32[]{:S(2)}) copy-start(f32[2,1024,32]{1,2,0:T(8,128)} %param.55) | copy-start | bytes 786436
  238.7 11.3 %copy-start.3 = (f32[2,32,1024]{2,1,0:T(8,128)S(1)}, f32[2,32,1024]{2,1,0:T(8,128)}, u32[]{:S(2)}) copy-start(f32[2,32,1024]{2,1,0:T(8,128)} %refs_2_.1) | copy-start | bytes 786436
  238.7 11.3 %copy-start.10 = (f32[2,32,1024]{2,1,0:T(8,128)S(1)}, f32[2,32,1024]{2,1,0:T(8,128)}, u32[]{:S(2)}) copy-start(f32[2,32,1024]{2,1,0:T(8,128)} %param.46) | copy-start | bytes 786436
  238.7 11.3 %copy-start.11 = (f32[2,32,1024]{2,1,0:T(8,128)S(1)}, f32[2,32,1024]{2,1,0:T(8,128)}, u32[]{:S(2)}) copy-start(f32[2,32,1024]{2,1,0:T(8,128)} %param.54) | copy-start | bytes 786436
  247.0 4.0 %copy-start.1 = (f32[6,196,512]{2,1,0:T(8,128)S(1)}, f32[6,196,512]{2,1,0:T(8,128)}, u32[]{:S(2)}) copy-start(f32[6,196,512]{2,1,0:T(8,128)} %get-tuple-element.56) | copy-start | bytes 7225348
  253.3 2.8 %copy-start = (f32[6,196,512]{2,1,0:T(8,128)S(1)}, f32[6,196,512]{2,1,0:T(8,128)}, u32[]{:S(2)}) copy-start(f32[6,196,512]{2,1,0:T(8,128)} %get-tuple-element.46) | copy-start | bytes 7225348

commit v2 on v1

--- a/solution.py
+++ b/solution.py
@@ -192,8 +192,8 @@
     return x + attn + nv_ref[4:5, :]
 
 
-CH = 512
-SLOTS = 8
+CH = 1024
+SLOTS = 6
 LAG = 2
 SPAN = 12
 
@@ -212,7 +212,8 @@
             act_ref[:, col : col + CH] = act
             slope_ref[:, col : col + CH] = (phi + u * (jnp.exp2(t * t * -log2_e) * inv_root_two_pi)).astype(bf16)
             if col > 0:
-                at("mlp", col // CH)
+                for point in range(col // CH, 4 if col + CH == 2 * FFH else col // CH + 1):
+                    at("mlp", point)
             total += dot(act, flat(wm[m, ..., FFH + c : FFH + c + CH]), 1, 1)
     return mid + total + nv_ref[5:6, :]
 
@@ -232,7 +233,8 @@
             g = g.astype(bf16)
             gp[rows, col : col + CH] = g
             if col > 0:
-                at("mlp", col // CH)
+                for point in range(col // CH, 4 if col + CH == 2 * FFH else col // CH + 1):
+                    at("mlp", point)
             ghid += dot(g, flat(wm[m, ..., c : c + CH]), 1, 1)
     gmid = gout + norm_back(ghid, hat, inv, nv_ref[2:3, :])
     nv_acc[2:3, :] += row_sum(ghid * hat)
@@ -565,7 +567,7 @@
     return pl.BlockSpec(shape, lambda i: zero, pipeline_mode=pl.Buffered(buffers))
 
 
-VLIM = 65000000
+VLIM = 67000000
 
 
 def forward(tok, shards, bias, vecs, nv, perm, perm_t, hm, fast, steps):

time: 262 us -> 259 us (0.989)
  Pallas kernels: 225 us -> 222 us
    pallas_call x1, Pallas kernels: 105 us -> 102 us  [backward(): pl.pallas_call(functools.partial(backward_kernel, fast, steps), name='bac...]
where the time goes in v2:
time: 259 us; the launch traced here: 258 us
  Pallas kernels  222 us (86%)
  other arithmetic  24.8 us (10%)
  local copies, waits for them, and re-layouts  6.71 us (3%)
  matrix products  2.85 us (1%)
    pallas_call x1, Pallas kernels, backward(): pl.pallas_call(functools.partial(backward_kernel, fast, steps), name='bac...  102 us
    pallas_call x1, Pallas kernels, forward(): pl.pallas_call(functools.partial(forward_kernel, fast, steps), name='forw...  90.4 us
    pallas_call x1, Pallas kernels, tail(): pl.pallas_call(tail_kernel, name='tail', out_shape=[jax.ShapeDtypeStruct(...  29.2 us
    sub x8, other arithmetic, adam_update(): weight_in - learn_rate * (hat_one / (jnp.sqrt(hat_two) + adam_eps) + deca...  11.3 us
    concatenate x2, other arithmetic, both_halves(): return jnp.concatenate([low, high], 0)  5.6 us
  transfers between devices with their start and end apart: 2, of which 0 were waited for; matrix products, arithmetic and copies ran while one was open for 9% of the time, Pallas kernels for 11%

profile of v2, /device:TPU:0, one launch (start us, length us, event | category | flops | bytes accessed | tf_op | source)
XLA Modules:
  0.0 258.4 jit_solution(12995340377479377380)
XLA Ops:
  0.7 0.7 fusion.35
  1.4 0.8 copy.99
  2.2 1.2 fusion.8
  3.4 0.0 copy-start.9
  3.4 0.1 slice_add_fusion
  3.5 0.0 copy-start.10
  3.5 0.0 copy-start.15
  3.6 0.1 copy.113
  3.7 0.3 concatenate.23
  4.0 0.2 concatenate.24
  4.2 0.1 copy-done.9
  4.3 0.1 add.178
  4.5 0.4 add.179
  4.9 0.6 copy.87.refs_6_.nv_ref
  6.2 0.6 select_maximum_fusion.refs_5_
  6.8 0.9 fusion.14.refs_4_
  7.7 90.4 %forward.1 = (f32[6,196,512]{2,1,0:T(8,128)}, f32[1200,512]{1,0:T(8,128)}, f32[2400,512]{1,0:T(8,128)}, bf16[3072,1536]{1,0:T(8,128)(2,1)}, bf16[2400,512]{1,0:T...) custom-call(bf16[12,196,512]{2,1,0:T(8,128)(2,1)} %tok_ref.3, ...), custom_call_target="tpu_custom_call" | custom-call | tf_op jit(solution)/shard_map/forward/pallas_call | solution.py:592
  98.2 102.1 %backward.1 = (f32[6,196,512]{2,1,0:T(8,128)}, bf16[2,4,2,2,32,1024]{5,4,3,2,1,0:T(8,128)(2,1)}, f32[2,2,32,1024]{3,2,1,0:T(8,128)}, f32[1,32,1024]{2,1,0:T(8,12...) custom-call(f32[12,196,512]{2,1,0:T(8,128)} %cot_ref.1, ...), custom_call_target="tpu_custom_call" | custom-call | tf_op jit(solution)/shard_map/backward/pallas_call | solution.py:669
  200.3 0.1 collective-permute-start.1
  200.4 0.5 collective-permute-start
  200.9 1.5 reshape.179
  202.4 1.7 fusion.11
  204.1 0.0 copy-start.11
  204.1 0.1 reshape.180
  204.3 0.1 concatenate.29
  204.5 0.1 reshape.182
  204.6 0.6 pad_bitcast_fusion.small_ref
  205.2 29.2 %tail.1 = (f32[32,1024]{1,0:T(8,128)}, f32[144,128]{1,0:T(8,128)}) custom-call(bf16[2,4,2,2,32,1024]{5,4,3,2,1,0:T(8,128)(2,1)} %get-tuple-element.57.grad_ref, f32[144,128]{1,0:T(8,128)} %pad_bitcast_fusion.small_ref), custom_call_target="tpu_custom_call" | custom-call | tf_op jit(solution)/shard_map/tail/pallas_call | solution.py:1049
  234.4 0.0 copy-start.2
  234.5 0.0 copy-start.6
  234.5 1.1 reshape.186
  235.6 0.0 copy-start.7
  235.6 0.0 copy-start.8
  235.6 0.1 slice.68
  235.7 0.1 reshape.189
  235.9 1.0 fusion.19
  236.8 1.4 multiply_subtract_fusion.6
  238.2 1.3 multiply_subtract_fusion.7
  239.6 1.4 multiply_subtract_fusion.5
  240.9 1.5 multiply_subtract_fusion.4
  242.4 1.6 multiply_subtract_fusion.3
  244.0 2.2 multiply_subtract_fusion.2
  246.2 1.0 multiply_subtract_fusion
  247.2 1.0 multiply_subtract_fusion.1
  248.2 2.3 broadcast_select_fusion.1
  250.5 2.8 %pad_maximum_fusion.1 = f32[12,196,512]{2,1,0:T(8,128)} fusion(f32[6,196,512]{2,1,0:T(8,128)S(1)} %get-tuple-element.117, f32[6,196,512]{2,1,0:T(8,128)S(1)} %get-tuple-element.116), kind=kLoop, calls=%fused_computation.1 | loop fusion | flops 1204224 | bytes 9633792 | tf_op jit(solution)/shard_map/concatenate | solution.py:1074
  253.3 2.3 broadcast_select_fusion.3
  255.6 2.8 %pad_maximum_fusion = f32[12,196,512]{2,1,0:T(8,128)} fusion(f32[6,196,512]{2,1,0:T(8,128)S(1)} %get-tuple-element.119, f32[6,196,512]{2,1,0:T(8,128)S(1)} %get-tuple-element.118), kind=kLoop, calls=%fused_computation | loop fusion | flops 1204224 | bytes 9633792 | tf_op jit(solution)/shard_map/concatenate | solution.py:1074
  (41 shorter events, 0.2 us)
Async XLA Ops:
  3.4 0.9 copy-start.9
  3.5 1.3 copy-start.10
  3.5 2.0 copy-start.13
  3.5 2.6 %copy-start.15 = (f32[2,2,256]{2,1,0:T(2,128)S(1)}, f32[2,2,256]{2,1,0:T(2,128)}, u32[]{:S(2)}) copy-start(f32[2,2,256]{2,1,0:T(2,128)} %param.40) | copy-start | bytes 12292
  200.3 3.9 %copy-start.14 = (f32[2,8,512]{2,1,0:T(8,128)S(1)}, f32[2,8,512]{2,1,0:T(8,128)}, u32[]{:S(2)}) copy-start(f32[2,8,512]{2,1,0:T(8,128)} %get-tuple-element.61) | copy-start | bytes 98308
  200.3 4.0 %copy-start.16 = (f32[2,1,2048]{2,1,0:T(1,128)S(1)}, f32[2,1,2048]{2,1,0:T(1,128)}, u32[]{:S(2)}) copy-start(f32[2,1,2048]{2,1,0:T(1,128)} %get-tuple-element.59) | copy-start | bytes 49156
  200.3 4.0 %copy-start.17 = (f32[2,2,512]{2,1,0:T(2,128)S(1)}, f32[2,2,512]{2,1,0:T(2,128)}, u32[]{:S(2)}) copy-start(f32[2,2,512]{2,1,0:T(2,128)} %get-tuple-element.58) | copy-start | bytes 24580
  200.3 47.9 %collective-permute-start.1 = (f32[6,196,512]{2,1,0:T(8,128)}, f32[6,196,512]{2,1,0:T(8,128)}, u32[]{:S(2)}, u32[]{:S(2)}) collective-permute-start(f32[6,196,512]{2,1,0:T(8,128)} %get-tuple-element.56), channel_id=1, source_target_pairs={{0,1},{1,0},{2,3},{3,2},{4,5},{5,4},{6,7},{7,6},{8,9},{9,8},{10,11... | collective-permute-start | bytes 7225352 | tf_op jit(solution)/shard_map/ppermute | solution.py:1071
  200.4 52.9 %collective-permute-start = (f32[6,196,512]{2,1,0:T(8,128)}, f32[6,196,512]{2,1,0:T(8,128)}, u32[]{:S(2)}, u32[]{:S(2)}) collective-permute-start(f32[6,196,512]{2,1,0:T(8,128)} %get-tuple-element.46), channel_id=1, source_target_pairs={{0,1},{1,0},{2,3},{3,2},{4,5},{5,4},{6,7},{7,6},{8,9},{9,8},{10,11... | collective-permute-start | bytes 7225352 | tf_op jit(solution)/shard_map/ppermute | solution.py:1071
  204.1 35.5 %copy-start.12 = (f32[2,169,8]{1,2,0:T(8,128)S(1)}, f32[2,169,8]{1,2,0:T(8,128)}, u32[]{:S(2)}) copy-start(f32[2,169,8]{1,2,0:T(8,128)} %param.42) | copy-start | bytes 32452
  204.1 36.8 %copy-start.11 = (f32[2,6,512]{2,0,1:T(2,128)S(1)}, f32[2,6,512]{2,0,1:T(2,128)}, u32[]{:S(2)}) copy-start(f32[2,6,512]{2,0,1:T(2,128)} %param.43) | copy-start | bytes 73732
  234.4 11.8 %copy-start.2 = (f32[2,1024,32]{1,2,0:T(8,128)S(1)}, f32[2,1024,32]{1,2,0:T(8,128)}, u32[]{:S(2)}) copy-start(f32[2,1024,32]{1,2,0:T(8,128)} %param.39) | copy-start | bytes 786436
  234.4 11.7 %copy-start.4 = (f32[2,2,32,1024]{3,2,1,0:T(8,128)S(1)}, f32[2,2,32,1024]{3,2,1,0:T(8,128)}, u32[]{:S(2)}) copy-start(f32[2,2,32,1024]{3,2,1,0:T(8,128)} %get-tuple-element.64) | copy-start | bytes 1572868
  234.4 11.7 %copy-start.5 = (f32[2,1024,32]{1,2,0:T(8,128)S(1)}, f32[2,1024,32]{1,2,0:T(8,128)}, u32[]{:S(2)}) copy-start(f32[2,1024,32]{1,2,0:T(8,128)} %param.47) | copy-start | bytes 786436
  234.5 11.7 %copy-start.6 = (f32[2,1024,32]{1,2,0:T(8,128)S(1)}, f32[2,1024,32]{1,2,0:T(8,128)}, u32[]{:S(2)}) copy-start(f32[2,1024,32]{1,2,0:T(8,128)} %param.55) | copy-start | bytes 786436
  235.6 11.6 %copy-start.3 = (f32[2,32,1024]{2,1,0:T(8,128)S(1)}, f32[2,32,1024]{2,1,0:T(8,128)}, u32[]{:S(2)}) copy-start(f32[2,32,1024]{2,1,0:T(8,128)} %refs_2_.1) | copy-start | bytes 786436
  235.6 11.6 %copy-start.7 = (f32[2,32,1024]{2,1,0:T(8,128)S(1)}, f32[2,32,1024]{2,1,0:T(8,128)}, u32[]{:S(2)}) copy-start(f32[2,32,1024]{2,1,0:T(8,128)} %param.46) | copy-start | bytes 786436
  235.6 11.6 %copy-start.8 = (f32[2,32,1024]{2,1,0:T(8,128)S(1)}, f32[2,32,1024]{2,1,0:T(8,128)}, u32[]{:S(2)}) copy-start(f32[2,32,1024]{2,1,0:T(8,128)} %param.54) | copy-start | bytes 786436
  244.0 4.2 %copy-start.1 = (f32[6,196,512]{2,1,0:T(8,128)S(1)}, f32[6,196,512]{2,1,0:T(8,128)}, u32[]{:S(2)}) copy-start(f32[6,196,512]{2,1,0:T(8,128)} %get-tuple-element.56) | copy-start | bytes 7225348
  250.5 2.8 %copy-start = (f32[6,196,512]{2,1,0:T(8,128)S(1)}, f32[6,196,512]{2,1,0:T(8,128)}, u32[]{:S(2)}) copy-start(f32[6,196,512]{2,1,0:T(8,128)} %get-tuple-element.46) | copy-start | bytes 7225348
